TPU v7x, 32 devices: a whole 2x2x4 slice. The times are simulated.
32 devices in a mesh: pb: 4 (over x, core), kv: 8 (over z, y).
Axes of the slice: x: 2, y: 2, z: 4, core: 2. Of those that a mesh axis runs over, the one named last changes fastest.
Arguments:
- queries: bfloat16 [32768, 256], P(('pb', 'kv')), may hold values from -64 to 64
- keys: bfloat16 [1024, 256], P('kv'), may hold values from -6 to 6
- values: bfloat16 [1024, 256], P('kv'), may hold values from -6 to 6
- dout: bfloat16 [32768, 256], P(('pb', 'kv')), may hold values from -256 to 256
Outputs:
- dq: float32 [32768, 256], P(('pb', 'kv'))
- dk: float32 [1024, 256], P('kv')
- dv: float32 [1024, 256], P('kv')
All inputs are finite; a program needn't handle non-finite values.
Results may differ from a plain program's by a relative error of at most 0.0029.
Values may be sent and summed in bfloat16 or wider, within the bound.
No kernel may reach another device: no remote copies, remote signals or barrier semaphores. Data moves between devices by JAX's collectives and lax.ppermute only.
A program may use at most 64 MiB of HBM per device.

v0:
```python
import math

import jax
import jax.numpy as jnp
from jax import lax
from jax.experimental import pallas as pl
from jax.experimental.pallas import tpu as pltpu
from jax.sharding import PartitionSpec as P


H = 2
DH = 128
W = H * DH


def swap(x, axis, bit):
    n = lax.axis_size(axis)
    return lax.ppermute(x, axis, [(i, i ^ bit) for i in range(n)])


def shift(x, axis, by):
    n = lax.axis_size(axis)
    return lax.ppermute(x, axis, [(i, (i + by) % n) for i in range(n)])


def dot(a, b):
    return lax.dot_general(a, b, (((1,), (0,)), ((), ())), preferred_element_type=jnp.float32)


def score_kernel(to_exp2, qt_ref, dot_ref, kv_ref, p_ref, dp_ref, stat_ref):
    rows = kv_ref.shape[0]
    for h in range(H):
        head = slice(h * DH, (h + 1) * DH)
        vhead = slice(W + h * DH, W + (h + 1) * DH)
        own = slice(h * rows, (h + 1) * rows)
        s = dot(kv_ref[:, head], qt_ref[head, :]) * to_exp2
        peak = jnp.max(s, axis=0, keepdims=True)
        p = jnp.exp2(s - peak)
        dp = dot(kv_ref[:, vhead], dot_ref[head, :])
        p_ref[own, :] = p
        dp_ref[own, :] = dp
        stat_ref[h : h + 1, :] = peak
        stat_ref[H + h : H + h + 1, :] = jnp.sum(p, axis=0, keepdims=True)
        stat_ref[2 * H + h : 2 * H + h + 1, :] = jnp.sum(p * dp, axis=0, keepdims=True)


def score(queries_t, dout_t, kv):
    rows, n = kv.shape[0], queries_t.shape[1]
    vmem = pl.BlockSpec(memory_space=pltpu.VMEM)
    big = jax.ShapeDtypeStruct((H * rows, n), jnp.float32)
    return pl.pallas_call(
        lambda *refs: score_kernel(math.log2(math.e) / math.sqrt(DH), *refs),
        in_specs=[vmem] * 3,
        out_specs=[vmem] * 3,
        out_shape=[big, big, jax.ShapeDtypeStruct((4 * H, n), jnp.float32)],
        compiler_params=pltpu.CompilerParams(vmem_limit_bytes=12 * 2**20),
        cost_estimate=pl.CostEstimate(
            flops=4 * n * rows * W, bytes_accessed=8 * n * W, transcendentals=0
        ),
    )(queries_t, dout_t, kv)


def attn_kernel(sizes, groups, early, block, *refs):
    q_ref, do_ref, qt_ref, dot_ref = refs[:4]
    pieces = refs[4 : 4 + len(sizes)]
    refs = refs[4 + len(sizes) :]
    scored = {at: refs[3 * e : 3 * e + 3] for e, at in enumerate(early)}
    refs = refs[3 * len(early) :]
    dq_ref = refs[0]
    outs = refs[1 : 1 + len(groups)]
    kv_ref, kt_ref, p_ref, dp_ref = refs[1 + len(groups) :]
    total = sum(sizes)
    scale = 1.0 / math.sqrt(DH)
    to_exp2 = scale * math.log2(math.e)
    step = pl.program_id(0)
    last = pl.num_programs(0) - 1
    spans = [slice(at, at + block) for at in range(0, total, block)]
    places = [
        (i, outs[i], slice(at, at + block))
        for i, g in enumerate(groups)
        for at in range(0, g, block)
    ]
    fresh = [span for span, place in zip(spans, places) if place[0] not in scored]

    @pl.when(step == 0)
    def _():
        at = 0
        for piece, rows in zip(pieces, sizes):
            kv_ref[at : at + rows, :] = piece[...]
            at += rows
        for out in outs:
            out[...] = jnp.zeros_like(out)
        for span in spans:
            kt_ref[:, span] = kv_ref[span, :W].T

    for h in range(H):
        head = slice(h * DH, (h + 1) * DH)
        vhead = slice(W + h * DH, W + (h + 1) * DH)
        peak = None
        for span in fresh:
            s = dot(kv_ref[span, head], qt_ref[head, :]) * to_exp2
            p_ref[span, :] = s
            m = jnp.max(s, axis=0, keepdims=True)
            peak = m if peak is None else jnp.maximum(peak, m)
        for _, _, stat in scored.values():
            peak = jnp.maximum(peak, stat[h : h + 1, :])
        mass = jnp.zeros_like(peak)
        weighted = jnp.zeros_like(peak)
        share = {}
        for i, (_, _, stat) in scored.items():
            share[i] = jnp.exp2(stat[h : h + 1, :] - peak)
            mass = mass + share[i] * stat[H + h : H + h + 1, :]
            weighted = weighted + share[i] * stat[2 * H + h : 2 * H + h + 1, :]
        for span in fresh:
            dp = dot(kv_ref[span, vhead], dot_ref[head, :])
            p = jnp.exp2(p_ref[span, :] - peak)
            p_ref[span, :] = p
            dp_ref[span, :] = dp
            mass = mass + jnp.sum(p, axis=0, keepdims=True)
            weighted = weighted + jnp.sum(p * dp, axis=0, keepdims=True)
        inv = 1.0 / mass
        delta = weighted * inv
        dq = None
        for span, (i, out, part_rows) in zip(spans, places):
            if i in scored:
                at = h * groups[i] + part_rows.start
                there = slice(at, at + block)
                p = scored[i][0][there, :] * (share[i] * inv)
                dp = scored[i][1][there, :]
            else:
                p = p_ref[span, :] * inv
                dp = dp_ref[span, :]
            ds = (p * (dp - delta)).astype(jnp.bfloat16)
            out[part_rows, vhead] += dot(p.astype(jnp.bfloat16), do_ref[:, head])
            out[part_rows, head] += dot(ds, q_ref[:, head])
            part = dot(kt_ref[head, span], ds)
            dq = part if dq is None else dq + part
        dq_ref[head, :] = dq * scale

    @pl.when(step == last)
    def _():
        for out in outs:
            out[:, :W] = out[:, :W] * scale


def attn(queries, dout, queries_t, dout_t, pieces, groups, scored):
    rows_q = queries.shape[0]
    sizes = [p.shape[0] for p in pieces]
    total = sum(sizes)
    tile = math.gcd(rows_q, 1024 if total <= 1024 else 256)
    block = math.gcd(groups[0], 256)
    limit = 8 * total * tile + 6 * total * W + 20 * tile * W + 8 * 2**20
    row = pl.BlockSpec((tile, W), lambda i: (i, 0))
    col = pl.BlockSpec((W, tile), lambda i: (0, i))
    vmem = pl.BlockSpec(memory_space=pltpu.VMEM)
    return pl.pallas_call(
        lambda *refs: attn_kernel(sizes, groups, list(scored), block, *refs),
        grid=(rows_q // tile,),
        in_specs=[row, row, col, col]
        + [pl.BlockSpec(p.shape, lambda i: (0, 0)) for p in pieces]
        + [vmem] * (3 * len(scored)),
        out_specs=[col] + [vmem] * len(groups),
        out_shape=[jax.ShapeDtypeStruct((W, rows_q), jnp.float32)]
        + [jax.ShapeDtypeStruct((g, 2 * W), jnp.float32) for g in groups],
        scratch_shapes=[
            pltpu.VMEM((total, 2 * W), jnp.bfloat16),
            pltpu.VMEM((W, total), jnp.bfloat16),
            pltpu.VMEM((total, tile), jnp.float32),
            pltpu.VMEM((total, tile), jnp.float32),
        ],
        compiler_params=pltpu.CompilerParams(vmem_limit_bytes=limit),
        cost_estimate=pl.CostEstimate(
            flops=10 * rows_q * total * W, bytes_accessed=8 * rows_q * W, transcendentals=0
        ),
    )(queries, dout, queries_t, dout_t, *pieces, *[x for triple in scored.values() for x in triple])


def hops(lines):
    return sorted(range(1, lines), key=lambda j: (-min(j, lines - j), j))


def program(queries, keys, values, dout):
    lines = lax.axis_size("kv") // 2
    core = lax.axis_index("pb") % 2
    half = keys.shape[0] // 2
    kv = jnp.concatenate([keys, values], axis=1)
    mine = lax.dynamic_slice_in_dim(kv, core * half, half, 0)
    order = hops(lines)
    near = [mine] + [shift(mine, "kv", 2 * j) for j in order]
    near[-1], queries_t, dout_t = lax.optimization_barrier((near[-1], queries.T, dout.T))
    far = []
    for piece in near:
        far.append(swap(piece, "kv", 1))
    near = jnp.concatenate(near, axis=0)
    near_o = swap(near, "pb", 1)
    many = lines * half
    scored = {}
    early = 4 * many <= queries.shape[0]
    if early:
        scored[3] = score(queries_t, dout_t, near)
        far[-1], _ = lax.optimization_barrier((far[-1], scored[3][2]))
    far_all = jnp.concatenate(far, axis=0)
    far_o = swap(far_all, "pb", 1)

    if early:
        late, _ = lax.optimization_barrier((near_o, far_all))
        scored[1] = score(queries_t, dout_t, late)
    dq, g_far_o, g_near_o, g_far, g_near = attn(
        queries, dout, queries_t, dout_t, [far_o, near_o, far_all, near], [many] * 4, scored
    )
    g_far_o = swap(g_far_o, "pb", 1)
    g_near_o = swap(g_near_o, "pb", 1)

    def rows(x, k):
        return x[k * half : (k + 1) * half]

    def from_far(k):
        sent = (rows(g_far, k) + rows(g_far_o, k)).astype(jnp.bfloat16)
        return swap(sent, "kv", 1)

    arrived = {k: from_far(k) for k in range(1, lines)}
    g_far, _ = lax.optimization_barrier((g_far, arrived[1]))
    arrived[0] = from_far(0)

    def merged(k):
        return rows(g_near, k) + rows(g_near_o, k) + arrived[k].astype(jnp.float32)

    parts = []
    for k, j in enumerate(order, 1):
        sent = merged(k).astype(jnp.bfloat16)
        parts.append(shift(sent, "kv", -2 * j))
        after = (k + 1) % lines
        arrived[after], _ = lax.optimization_barrier((arrived[after], sent))
    total = merged(0)
    for part in parts:
        total = total + part.astype(jnp.float32)
    for bit in range(1, lax.axis_size("pb").bit_length() - 1):
        total = total + swap(total, "pb", 1 << bit)
    other = swap(total, "pb", 1)
    first = jnp.where(core == 0, total, other)
    second = jnp.where(core == 0, other, total)
    both = jnp.concatenate([first, second], axis=0)
    return (dq.T, both[:, :W], both[:, W:])


def solution(mesh):
    return jax.shard_map(
        program,
        mesh=mesh,
        in_specs=(P(("pb", "kv"), None), P("kv", None), P("kv", None), P(("pb", "kv"), None)),
        out_specs=(P(("pb", "kv"), None), P("kv", None), P("kv", None)),
        check_vma=False,
    )
```

profile of v0, /device:TPU:0, one launch (start us, length us, event | category | flops | bytes accessed | tf_op | source)
XLA Modules:
  0.0 53.4 jit_solution(12660877663213738696)
XLA Ops:
  0.6 0.8 %fusion.15 = bf16[64,512]{1,0:T(8,128)(2,1)S(1)} fusion(s32[]{:T(128)S(6)} %select_n.23, bf16[128,256]{1,0:T(8,128)(2,1)} %param.5, bf16[128,256]{1,0:T(8,128)(2,1)} %param.6), kind=kLoop, calls=%fused_computation.29 | loop fusion | flops 131072 | bytes 196612 | tf_op jit(solution)/shard_map/concatenate | solution.py:186
  1.4 5.1 %collective-permute-start = (bf16[64,512]{1,0:T(8,128)(2,1)S(1)}, bf16[64,512]{1,0:T(8,128)(2,1)S(1)}, u32[]{:S(2)}, u32[]{:S(2)}) collective-permute-start(bf16[64,512]{1,0:T(8,128)(2,1)S(1)} %fusion.15), channel_id=1, source_target_pairs={{0,6},{1,7},{2,0},{3,1},{4,2},{5,3},{6,4},{7,5},{8,14},{9,15},{10,... | collective-permute-start | bytes 196616 | tf_op jit(solution)/shard_map/ppermute | solution.py:23
  6.5 0.0 collective-permute-start.4
  6.5 1.0 %collective-permute-start.2 = (bf16[64,512]{1,0:T(8,128)(2,1)S(1)}, bf16[64,512]{1,0:T(8,128)(2,1)S(1)}, u32[]{:S(2)}, u32[]{:S(2)}) collective-permute-start(bf16[64,512]{1,0:T(8,128)(2,1)S(1)} %fusion.15), channel_id=1, source_target_pairs={{0,4},{1,5},{2,6},{3,7},{4,0},{5,1},{6,2},{7,3},{8,12},{9,13},{10,... | collective-permute-start | bytes 196616 | tf_op jit(solution)/shard_map/ppermute | solution.py:23
  7.5 1.5 %collective-permute-start.1 = (bf16[64,512]{1,0:T(8,128)(2,1)S(1)}, bf16[64,512]{1,0:T(8,128)(2,1)S(1)}, u32[]{:S(2)}, u32[]{:S(2)}) collective-permute-start(bf16[64,512]{1,0:T(8,128)(2,1)S(1)} %fusion.15), channel_id=1, source_target_pairs={{0,1},{1,0},{2,3},{3,2},{4,5},{5,4},{6,7},{7,6},{8,9},{9,8},{10,11... | collective-permute-start | bytes 196616 | tf_op jit(solution)/shard_map/ppermute | solution.py:18
  9.0 1.2 %copy.7 = bf16[1024,256]{0,1:T(8,128)(2,1)S(1)} copy(bf16[1024,256]{1,0:T(8,128)(2,1)} %refs_0_.1) | data formatting | bytes 1048576 | tf_op args[0]
  10.3 1.2 %copy.8 = bf16[1024,256]{0,1:T(8,128)(2,1)S(1)} copy(bf16[1024,256]{1,0:T(8,128)(2,1)} %refs_1_.1) | data formatting | bytes 1048576 | tf_op args[3]
  11.5 0.0 copy-start
  11.6 0.0 copy-start.1
  11.6 0.0 collective-permute-done
  11.6 0.6 %collective-permute-start.6 = (bf16[64,512]{1,0:T(8,128)(2,1)S(1)}, bf16[64,512]{1,0:T(8,128)(2,1)S(1)}, u32[]{:S(2)}, u32[]{:S(2)}) collective-permute-start(bf16[64,512]{1,0:T(8,128)(2,1)S(1)} %collective-permute-done), channel_id=1, source_target_pairs={{0,1},{1,0},{2,3},{3,2},{4,5},{5,4},{6,7},{7,6},{8,9},{9,8},{10,11... | collective-permute-start | bytes 196616 | tf_op jit(solution)/shard_map/ppermute | solution.py:18
  12.2 0.5 collective-permute-done.4
  12.7 1.3 %collective-permute-done.2 = bf16[64,512]{1,0:T(8,128)(2,1)S(1)} collective-permute-done((bf16[64,512]{1,0:T(8,128)(2,1)S(1)}, bf16[64,512]{1,0:T(8,128)(2,1)S(1)}, u32[]{:S(2)}, u32[]{:S(2)}) %collective-permute-start.2) | collective-permute-done | bytes 65568 | tf_op jit(solution)/shard_map/ppermute | solution.py:23
  14.0 0.1 collective-permute-start.8
  14.1 1.6 %collective-permute-start.5 = (bf16[64,512]{1,0:T(8,128)(2,1)S(1)}, bf16[64,512]{1,0:T(8,128)(2,1)S(1)}, u32[]{:S(2)}, u32[]{:S(2)}) collective-permute-start(bf16[64,512]{1,0:T(8,128)(2,1)S(1)} %collective-permute-done.4), channel_id=1, source_target_pairs={{0,1},{1,0},{2,3},{3,2},{4,5},{5,4},{6,7},{7,6},{8,9},{9,8},{10,11... | collective-permute-start | bytes 196616 | tf_op jit(solution)/shard_map/ppermute | solution.py:18
  15.7 0.5 collective-permute-start.3
  16.2 0.0 collective-permute-done.1
  16.2 0.9 %shard_map.67 = (f32[512,1024]{1,0:T(8,128)S(1)}, f32[512,1024]{1,0:T(8,128)S(1)}, f32[8,1024]{1,0:T(8,128)S(1)}) custom-call(bf16[256,1024]{1,0:T(8,128)(2,1)S(1)} %bitcast.3, bf16[256,1024]{1,0:T(8,128)(2,1)S(1)} %bitcast.6, bf16[256,512]{1,0:T(8,128)(2,1)S(1)} %pad_maximum_fusion.refs_2_.refs_7_), custom_call_target="tpu_custom_call" | custom-call | flops 268435456 | bytes 2097152 | tf_op jit(solution)/shard_map/pallas_call | solution.py:51
  17.0 0.0 collective-permute-done.6
  17.0 2.9 %collective-permute-done.3 = bf16[64,512]{1,0:T(8,128)(2,1)S(1)} collective-permute-done((bf16[64,512]{1,0:T(8,128)(2,1)S(1)}, bf16[64,512]{1,0:T(8,128)(2,1)S(1)}, u32[]{:S(2)}, u32[]{:S(2)}) %collective-permute-start.3) | collective-permute-done | bytes 65568 | tf_op jit(solution)/shard_map/ppermute | solution.py:18
  20.0 0.0 collective-permute-done.5
  20.0 0.1 collective-permute-start.7
  20.1 0.0 collective-permute-done.8.refs_2_.refs_5_
  20.1 0.9 %shard_map.68 = (f32[512,1024]{1,0:T(8,128)S(1)}, f32[512,1024]{1,0:T(8,128)S(1)}, f32[8,1024]{1,0:T(8,128)S(1)}) custom-call(bf16[256,1024]{1,0:T(8,128)(2,1)S(1)} %bitcast.4, bf16[256,1024]{1,0:T(8,128)(2,1)S(1)} %bitcast.7, bf16[256,512]{1,0:T(8,128)(2,1)S(1)} %collective-permute-done.8.refs_2_.refs_5_), custom_call_target="tpu_custom_call" | custom-call | flops 268435456 | bytes 2097152 | tf_op jit(solution)/shard_map/pallas_call | solution.py:51
  21.0 0.7 %collective-permute-done.7.refs_4_ = bf16[256,512]{1,0:T(8,128)(2,1)S(1)} collective-permute-done((bf16[256,512]{1,0:T(8,128)(2,1)S(1)}, bf16[256,512]{1,0:T(8,128)(2,1)S(1)}, u32[]{:S(2)}, u32[]{:S(2)}) %collective-permute-start.7) | collective-permute-done | bytes 262176 | tf_op jit(solution)/shard_map/ppermute | solution.py:18
  21.6 5.6 %shard_map.69 = (f32[256,1024]{1,0:T(8,128)S(1)}, f32[256,512]{1,0:T(8,128)S(1)}, f32[256,512]{1,0:T(8,128)S(1)}, f32[256,512]{1,0:T(8,128)S(1)}, f32[256,512]{1,0:T(8,128)S(1)}) custom-call(bf16[1024,256]{1,0:T(8,128)(2,1)S(1)} %copy-done, bf16[1024,256]{1,0:T(8,128)(2,1)S(1)} %copy-done.1, bf16[256,1024]{1,0:T(8,128)(2,1)S(1)} %bitcast.5, ...), custom_call_target="tpu_custom_call" | custom-call | flops 2684354560 | bytes 2097152 | tf_op jit(solution)/shard_map/pallas_call | solution.py:156
  27.2 0.2 collective-permute-start.10
  27.4 0.4 collective-permute-start.9
  27.8 1.4 %collective-permute-done.10 = f32[256,512]{1,0:T(8,128)S(1)} collective-permute-done((f32[256,512]{1,0:T(8,128)S(1)}, f32[256,512]{1,0:T(8,128)S(1)}, u32[]{:S(2)}, u32[]{:S(2)}) %collective-permute-start.10) | collective-permute-done | bytes 524320 | tf_op jit(solution)/shard_map/ppermute | solution.py:18
  29.2 0.1 fusion.10
  29.2 1.6 %collective-permute-start.11 = (bf16[64,512]{1,0:T(8,128)(2,1)S(1)}, bf16[64,512]{1,0:T(8,128)(2,1)S(1)}, u32[]{:S(2)}, u32[]{:S(2)}) collective-permute-start(bf16[64,512]{1,0:T(8,128)(2,1)S(1)} %get-tuple-element.46), channel_id=1, source_target_pairs={{0,1},{1,0},{2,3},{3,2},{4,5},{5,4},{6,7},{7,6},{8,9},{9,8},{10,11... | collective-permute-start | bytes 196616 | tf_op jit(solution)/shard_map/ppermute | solution.py:18
  30.8 0.5 collective-permute-start.14
  31.3 1.5 %collective-permute-start.13 = (bf16[64,512]{1,0:T(8,128)(2,1)S(1)}, bf16[64,512]{1,0:T(8,128)(2,1)S(1)}, u32[]{:S(2)}, u32[]{:S(2)}) collective-permute-start(bf16[64,512]{1,0:T(8,128)(2,1)S(1)} %get-tuple-element.48), channel_id=1, source_target_pairs={{0,1},{1,0},{2,3},{3,2},{4,5},{5,4},{6,7},{7,6},{8,9},{9,8},{10,11... | collective-permute-start | bytes 196616 | tf_op jit(solution)/shard_map/ppermute | solution.py:18
  32.8 1.0 %collective-permute-done.11 = bf16[64,512]{1,0:T(8,128)(2,1)S(1)} collective-permute-done((bf16[64,512]{1,0:T(8,128)(2,1)S(1)}, bf16[64,512]{1,0:T(8,128)(2,1)S(1)}, u32[]{:S(2)}, u32[]{:S(2)}) %collective-permute-start.11) | collective-permute-done | bytes 65568 | tf_op jit(solution)/shard_map/ppermute | solution.py:18
  33.9 1.2 %collective-permute-start.15 = (bf16[64,512]{1,0:T(8,128)(2,1)S(1)}, bf16[64,512]{1,0:T(8,128)(2,1)S(1)}, u32[]{:S(2)}, u32[]{:S(2)}) collective-permute-start(bf16[64,512]{1,0:T(8,128)(2,1)S(1)} %fusion.2), channel_id=1, source_target_pairs={{0,4},{1,5},{2,6},{3,7},{4,0},{5,1},{6,2},{7,3},{8,12},{9,13},{10,... | collective-permute-start | bytes 196616 | tf_op jit(solution)/shard_map/ppermute | solution.py:23
  35.0 1.0 %collective-permute-start.12 = (bf16[64,512]{1,0:T(8,128)(2,1)S(1)}, bf16[64,512]{1,0:T(8,128)(2,1)S(1)}, u32[]{:S(2)}, u32[]{:S(2)}) collective-permute-start(bf16[64,512]{1,0:T(8,128)(2,1)S(1)} %fusion.9), channel_id=1, source_target_pairs={{0,1},{1,0},{2,3},{3,2},{4,5},{5,4},{6,7},{7,6},{8,9},{9,8},{10,11... | collective-permute-start | bytes 196616 | tf_op jit(solution)/shard_map/ppermute | solution.py:18
  36.1 3.9 %collective-permute-start.16 = (bf16[64,512]{1,0:T(8,128)(2,1)S(1)}, bf16[64,512]{1,0:T(8,128)(2,1)S(1)}, u32[]{:S(2)}, u32[]{:S(2)}) collective-permute-start(bf16[64,512]{1,0:T(8,128)(2,1)S(1)} %fusion.5), channel_id=1, source_target_pairs={{0,6},{1,7},{2,0},{3,1},{4,2},{5,3},{6,4},{7,5},{8,14},{9,15},{10,... | collective-permute-start | bytes 196616 | tf_op jit(solution)/shard_map/ppermute | solution.py:23
  40.0 0.0 collective-permute-done.13
  40.0 0.1 collective-permute-start.17
  40.1 0.0 collective-permute-done.15
  40.1 1.8 %collective-permute-done.16 = bf16[64,512]{1,0:T(8,128)(2,1)S(1)} collective-permute-done((bf16[64,512]{1,0:T(8,128)(2,1)S(1)}, bf16[64,512]{1,0:T(8,128)(2,1)S(1)}, u32[]{:S(2)}, u32[]{:S(2)}) %collective-permute-start.16) | collective-permute-done | bytes 65568 | tf_op jit(solution)/shard_map/ppermute | solution.py:23
  41.9 4.2 %collective-permute-done.17 = bf16[64,512]{1,0:T(8,128)(2,1)S(1)} collective-permute-done((bf16[64,512]{1,0:T(8,128)(2,1)S(1)}, bf16[64,512]{1,0:T(8,128)(2,1)S(1)}, u32[]{:S(2)}, u32[]{:S(2)}) %collective-permute-start.17) | collective-permute-done | bytes 65568 | tf_op jit(solution)/shard_map/ppermute | solution.py:23
  46.2 1.6 %collective-permute-start.18 = (f32[64,512]{1,0:T(8,128)S(1)}, f32[64,512]{1,0:T(8,128)S(1)}, u32[]{:S(2)}, u32[]{:S(2)}) collective-permute-start(f32[64,512]{1,0:T(8,128)S(1)} %fusion.14), channel_id=1, source_target_pairs={{0,16},{8,24},{16,0},{24,8},{1,17},{9,25},{17,1},{25,9},{2,18},{10... | collective-permute-start | bytes 393224 | tf_op jit(solution)/shard_map/ppermute | solution.py:18
  47.7 3.5 %collective-permute-done.18 = f32[64,512]{1,0:T(8,128)S(1)} collective-permute-done((f32[64,512]{1,0:T(8,128)S(1)}, f32[64,512]{1,0:T(8,128)S(1)}, u32[]{:S(2)}, u32[]{:S(2)}) %collective-permute-start.18) | collective-permute-done | bytes 131104 | tf_op jit(solution)/shard_map/ppermute | solution.py:18
  51.2 0.1 collective-permute-start.19
  51.3 1.3 %copy.9 = f32[1024,256]{1,0:T(8,128)} copy(f32[1024,256]{0,1:T(8,128)S(1)} %bitcast.9) | data formatting | bytes 2097152
  52.6 0.0 collective-permute-done.19
  52.7 0.7 %pad_maximum_fusion.1 = (f32[128,256]{1,0:T(8,128)}, f32[128,256]{1,0:T(8,128)}) fusion(f32[64,512]{1,0:T(8,128)S(1)} %get-tuple-element.51, f32[64,512]{1,0:T(8,128)S(1)} %get-tuple-element.52), kind=kLoop, calls=%fused_computation.4 | loop fusion | flops 65536 | bytes 524288 | tf_op jit(solution)/shard_map/concatenate | solution.py:242
  (17 shorter events, 0.2 us)
Async XLA Ops:
  1.4 10.1 %collective-permute-start = (bf16[64,512]{1,0:T(8,128)(2,1)S(1)}, bf16[64,512]{1,0:T(8,128)(2,1)S(1)}, u32[]{:S(2)}, u32[]{:S(2)}) collective-permute-start(bf16[64,512]{1,0:T(8,128)(2,1)S(1)} %fusion.15), channel_id=1, source_target_pairs={{0,6},{1,7},{2,0},{3,1},{4,2},{5,3},{6,4},{7,5},{8,14},{9,15},{10,... | collective-permute-start | bytes 196616 | tf_op jit(solution)/shard_map/ppermute | solution.py:23
  6.5 6.2 %collective-permute-start.4 = (bf16[64,512]{1,0:T(8,128)(2,1)S(1)}, bf16[64,512]{1,0:T(8,128)(2,1)S(1)}, u32[]{:S(2)}, u32[]{:S(2)}) collective-permute-start(bf16[64,512]{1,0:T(8,128)(2,1)S(1)} %fusion.15), channel_id=1, source_target_pairs={{0,2},{1,3},{2,4},{3,5},{4,6},{5,7},{6,0},{7,1},{8,10},{9,11},{10,... | collective-permute-start | bytes 196616 | tf_op jit(solution)/shard_map/ppermute | solution.py:23
  6.5 7.5 %collective-permute-start.2 = (bf16[64,512]{1,0:T(8,128)(2,1)S(1)}, bf16[64,512]{1,0:T(8,128)(2,1)S(1)}, u32[]{:S(2)}, u32[]{:S(2)}) collective-permute-start(bf16[64,512]{1,0:T(8,128)(2,1)S(1)} %fusion.15), channel_id=1, source_target_pairs={{0,4},{1,5},{2,6},{3,7},{4,0},{5,1},{6,2},{7,3},{8,12},{9,13},{10,... | collective-permute-start | bytes 196616 | tf_op jit(solution)/shard_map/ppermute | solution.py:23
  7.5 8.6 %collective-permute-start.1 = (bf16[64,512]{1,0:T(8,128)(2,1)S(1)}, bf16[64,512]{1,0:T(8,128)(2,1)S(1)}, u32[]{:S(2)}, u32[]{:S(2)}) collective-permute-start(bf16[64,512]{1,0:T(8,128)(2,1)S(1)} %fusion.15), channel_id=1, source_target_pairs={{0,1},{1,0},{2,3},{3,2},{4,5},{5,4},{6,7},{7,6},{8,9},{9,8},{10,11... | collective-permute-start | bytes 196616 | tf_op jit(solution)/shard_map/ppermute | solution.py:18
  11.5 10.1 %copy-start = (bf16[1024,256]{1,0:T(8,128)(2,1)S(1)}, bf16[1024,256]{1,0:T(8,128)(2,1)}, u32[]{:S(2)}) copy-start(bf16[1024,256]{1,0:T(8,128)(2,1)} %refs_0_.1) | copy-start | bytes 1572868
  11.6 10.1 %copy-start.1 = (bf16[1024,256]{1,0:T(8,128)(2,1)S(1)}, bf16[1024,256]{1,0:T(8,128)(2,1)}, u32[]{:S(2)}) copy-start(bf16[1024,256]{1,0:T(8,128)(2,1)} %refs_1_.1) | copy-start | bytes 1572868
  11.6 5.5 %collective-permute-start.6 = (bf16[64,512]{1,0:T(8,128)(2,1)S(1)}, bf16[64,512]{1,0:T(8,128)(2,1)S(1)}, u32[]{:S(2)}, u32[]{:S(2)}) collective-permute-start(bf16[64,512]{1,0:T(8,128)(2,1)S(1)} %collective-permute-done), channel_id=1, source_target_pairs={{0,1},{1,0},{2,3},{3,2},{4,5},{5,4},{6,7},{7,6},{8,9},{9,8},{10,11... | collective-permute-start | bytes 196616 | tf_op jit(solution)/shard_map/ppermute | solution.py:18
  14.0 6.1 %collective-permute-start.8 = (bf16[256,512]{1,0:T(8,128)(2,1)S(1)}, bf16[256,512]{1,0:T(8,128)(2,1)S(1)}, u32[]{:S(2)}, u32[]{:S(2)}) collective-permute-start(bf16[256,512]{1,0:T(8,128)(2,1)S(1)} %pad_maximum_fusion.refs_2_.refs_7_), channel_id=1, source_target_pairs={{0,8},{8,0},{16,24},{24,16},{1,9},{9,1},{17,25},{25,17},{2,10},{10... | collective-permute-start | bytes 786440 | tf_op jit(solution)/shard_map/ppermute | solution.py:18
  14.1 5.9 %collective-permute-start.5 = (bf16[64,512]{1,0:T(8,128)(2,1)S(1)}, bf16[64,512]{1,0:T(8,128)(2,1)S(1)}, u32[]{:S(2)}, u32[]{:S(2)}) collective-permute-start(bf16[64,512]{1,0:T(8,128)(2,1)S(1)} %collective-permute-done.4), channel_id=1, source_target_pairs={{0,1},{1,0},{2,3},{3,2},{4,5},{5,4},{6,7},{7,6},{8,9},{9,8},{10,11... | collective-permute-start | bytes 196616 | tf_op jit(solution)/shard_map/ppermute | solution.py:18
  15.7 4.3 %collective-permute-start.3 = (bf16[64,512]{1,0:T(8,128)(2,1)S(1)}, bf16[64,512]{1,0:T(8,128)(2,1)S(1)}, u32[]{:S(2)}, u32[]{:S(2)}) collective-permute-start(bf16[64,512]{1,0:T(8,128)(2,1)S(1)} %collective-permute-done.2), channel_id=1, source_target_pairs={{0,1},{1,0},{2,3},{3,2},{4,5},{5,4},{6,7},{7,6},{8,9},{9,8},{10,11... | collective-permute-start | bytes 196616 | tf_op jit(solution)/shard_map/ppermute | solution.py:18
  20.0 1.6 %collective-permute-start.7 = (bf16[256,512]{1,0:T(8,128)(2,1)S(1)}, bf16[256,512]{1,0:T(8,128)(2,1)S(1)}, u32[]{:S(2)}, u32[]{:S(2)}) collective-permute-start(bf16[256,512]{1,0:T(8,128)(2,1)S(1)} %constant_dynamic-update-slice_fusion.refs_6_), channel_id=1, source_target_pairs={{0,8},{8,0},{16,24},{24,16},{1,9},{9,1},{17,25},{25,17},{2,10},{10... | collective-permute-start | bytes 786440 | tf_op jit(solution)/shard_map/ppermute | solution.py:18
  27.2 2.0 %collective-permute-start.10 = (f32[256,512]{1,0:T(8,128)S(1)}, f32[256,512]{1,0:T(8,128)S(1)}, u32[]{:S(2)}, u32[]{:S(2)}) collective-permute-start(f32[256,512]{1,0:T(8,128)S(1)} %get-tuple-element.38), channel_id=1, source_target_pairs={{0,8},{8,0},{16,24},{24,16},{1,9},{9,1},{17,25},{25,17},{2,10},{10... | collective-permute-start | bytes 1572872 | tf_op jit(solution)/shard_map/ppermute | solution.py:18
  27.4 6.4 %collective-permute-start.9 = (f32[256,512]{1,0:T(8,128)S(1)}, f32[256,512]{1,0:T(8,128)S(1)}, u32[]{:S(2)}, u32[]{:S(2)}) collective-permute-start(f32[256,512]{1,0:T(8,128)S(1)} %get-tuple-element.36), channel_id=1, source_target_pairs={{0,8},{8,0},{16,24},{24,16},{1,9},{9,1},{17,25},{25,17},{2,10},{10... | collective-permute-start | bytes 1572872 | tf_op jit(solution)/shard_map/ppermute | solution.py:18
  29.2 4.6 %collective-permute-start.11 = (bf16[64,512]{1,0:T(8,128)(2,1)S(1)}, bf16[64,512]{1,0:T(8,128)(2,1)S(1)}, u32[]{:S(2)}, u32[]{:S(2)}) collective-permute-start(bf16[64,512]{1,0:T(8,128)(2,1)S(1)} %get-tuple-element.46), channel_id=1, source_target_pairs={{0,1},{1,0},{2,3},{3,2},{4,5},{5,4},{6,7},{7,6},{8,9},{9,8},{10,11... | collective-permute-start | bytes 196616 | tf_op jit(solution)/shard_map/ppermute | solution.py:18
  30.8 5.3 %collective-permute-start.14 = (bf16[64,512]{1,0:T(8,128)(2,1)S(1)}, bf16[64,512]{1,0:T(8,128)(2,1)S(1)}, u32[]{:S(2)}, u32[]{:S(2)}) collective-permute-start(bf16[64,512]{1,0:T(8,128)(2,1)S(1)} %get-tuple-element.47), channel_id=1, source_target_pairs={{0,1},{1,0},{2,3},{3,2},{4,5},{5,4},{6,7},{7,6},{8,9},{9,8},{10,11... | collective-permute-start | bytes 196616 | tf_op jit(solution)/shard_map/ppermute | solution.py:18
  31.3 8.7 %collective-permute-start.13 = (bf16[64,512]{1,0:T(8,128)(2,1)S(1)}, bf16[64,512]{1,0:T(8,128)(2,1)S(1)}, u32[]{:S(2)}, u32[]{:S(2)}) collective-permute-start(bf16[64,512]{1,0:T(8,128)(2,1)S(1)} %get-tuple-element.48), channel_id=1, source_target_pairs={{0,1},{1,0},{2,3},{3,2},{4,5},{5,4},{6,7},{7,6},{8,9},{9,8},{10,11... | collective-permute-start | bytes 196616 | tf_op jit(solution)/shard_map/ppermute | solution.py:18
  33.9 6.2 %collective-permute-start.15 = (bf16[64,512]{1,0:T(8,128)(2,1)S(1)}, bf16[64,512]{1,0:T(8,128)(2,1)S(1)}, u32[]{:S(2)}, u32[]{:S(2)}) collective-permute-start(bf16[64,512]{1,0:T(8,128)(2,1)S(1)} %fusion.2), channel_id=1, source_target_pairs={{0,4},{1,5},{2,6},{3,7},{4,0},{5,1},{6,2},{7,3},{8,12},{9,13},{10,... | collective-permute-start | bytes 196616 | tf_op jit(solution)/shard_map/ppermute | solution.py:23
  35.0 5.0 %collective-permute-start.12 = (bf16[64,512]{1,0:T(8,128)(2,1)S(1)}, bf16[64,512]{1,0:T(8,128)(2,1)S(1)}, u32[]{:S(2)}, u32[]{:S(2)}) collective-permute-start(bf16[64,512]{1,0:T(8,128)(2,1)S(1)} %fusion.9), channel_id=1, source_target_pairs={{0,1},{1,0},{2,3},{3,2},{4,5},{5,4},{6,7},{7,6},{8,9},{9,8},{10,11... | collective-permute-start | bytes 196616 | tf_op jit(solution)/shard_map/ppermute | solution.py:18
  36.1 5.8 %collective-permute-start.16 = (bf16[64,512]{1,0:T(8,128)(2,1)S(1)}, bf16[64,512]{1,0:T(8,128)(2,1)S(1)}, u32[]{:S(2)}, u32[]{:S(2)}) collective-permute-start(bf16[64,512]{1,0:T(8,128)(2,1)S(1)} %fusion.5), channel_id=1, source_target_pairs={{0,6},{1,7},{2,0},{3,1},{4,2},{5,3},{6,4},{7,5},{8,14},{9,15},{10,... | collective-permute-start | bytes 196616 | tf_op jit(solution)/shard_map/ppermute | solution.py:23
  40.0 6.1 %collective-permute-start.17 = (bf16[64,512]{1,0:T(8,128)(2,1)S(1)}, bf16[64,512]{1,0:T(8,128)(2,1)S(1)}, u32[]{:S(2)}, u32[]{:S(2)}) collective-permute-start(bf16[64,512]{1,0:T(8,128)(2,1)S(1)} %fusion.8), channel_id=1, source_target_pairs={{0,2},{1,3},{2,4},{3,5},{4,6},{5,7},{6,0},{7,1},{8,10},{9,11},{10,... | collective-permute-start | bytes 196616 | tf_op jit(solution)/shard_map/ppermute | solution.py:23
  46.2 5.0 %collective-permute-start.18 = (f32[64,512]{1,0:T(8,128)S(1)}, f32[64,512]{1,0:T(8,128)S(1)}, u32[]{:S(2)}, u32[]{:S(2)}) collective-permute-start(f32[64,512]{1,0:T(8,128)S(1)} %fusion.14), channel_id=1, source_target_pairs={{0,16},{8,24},{16,0},{24,8},{1,17},{9,25},{17,1},{25,9},{2,18},{10... | collective-permute-start | bytes 393224 | tf_op jit(solution)/shard_map/ppermute | solution.py:18
  51.2 1.4 %collective-permute-start.19 = (f32[64,512]{1,0:T(8,128)S(1)}, f32[64,512]{1,0:T(8,128)S(1)}, u32[]{:S(2)}, u32[]{:S(2)}) collective-permute-start(f32[64,512]{1,0:T(8,128)S(1)} %add.72), channel_id=1, source_target_pairs={{0,8},{8,0},{16,24},{24,16},{1,9},{9,1},{17,25},{25,17},{2,10},{10... | collective-permute-start | bytes 393224 | tf_op jit(solution)/shard_map/ppermute | solution.py:18
where the time goes:
time: 53.7 us; the launch traced here: 53.4 us
  starting transfers between devices  22.4 us (42%)
  waiting for transfers between devices  17.3 us (32%)
  Pallas kernels  7.28 us (14%)
  local copies, waits for them, and re-layouts  3.84 us (7%)
  other arithmetic  1.75 us (3%)
  between operations  0.84 us (2%)
    ppermute x6, starting transfers between devices, shift(): return lax.ppermute(x, axis, [(i, (i + by) % n) for i in range(n)])  11.2 us
    ppermute x14, starting transfers between devices, swap(): return lax.ppermute(x, axis, [(i, i ^ bit) for i in range(n)])  11.2 us
    ppermute x14, waiting for transfers between devices, swap(): return lax.ppermute(x, axis, [(i, i ^ bit) for i in range(n)])  9.49 us
    ppermute x6, waiting for transfers between devices, shift(): return lax.ppermute(x, axis, [(i, (i + by) % n) for i in range(n)])  7.85 us
    pallas_call x1, Pallas kernels, attn(): pl.pallas_call(lambda *refs: attn_kernel(sizes, groups, list(scored), blo...  5.57 us
    unnamed x10, local copies, waits for them, and re-layouts  3.83 us
    pallas_call x2, Pallas kernels, score(): pl.pallas_call(lambda *refs: score_kernel(math.log2(math.e) / math.sqrt(D...  1.71 us
  transfers between devices with their start and end apart: 20, of which 9 were waited for; matrix products, arithmetic and copies ran while one was open for 7% of the time, Pallas kernels for 3%

commit v1 on v0

--- a/solution.py
+++ b/solution.py
@@ -60,15 +60,59 @@
     )(queries_t, dout_t, kv)
 
 
-def attn_kernel(sizes, groups, early, block, *refs):
+def grad_kernel(*refs):
+    q_ref, do_ref, kv_ref, p_ref, dp_ref, own_ref, stat_ref, old_ref, dq_ref, out_ref = refs
+    rows = kv_ref.shape[0]
+    scale = 1.0 / math.sqrt(DH)
+    for h in range(H):
+        head = slice(h * DH, (h + 1) * DH)
+        vhead = slice(W + h * DH, W + (h + 1) * DH)
+        there = slice(h * rows, (h + 1) * rows)
+        inv = stat_ref[H + h : H + h + 1, :]
+        delta = stat_ref[2 * H + h : 2 * H + h + 1, :]
+        share = jnp.exp2(own_ref[h : h + 1, :] - stat_ref[h : h + 1, :])
+        p = p_ref[there, :] * (share * inv)
+        ds = (p * (dp_ref[there, :] - delta)).astype(jnp.bfloat16)
+        out_ref[:, vhead] = dot(p.astype(jnp.bfloat16), do_ref[:, head])
+        out_ref[:, head] = dot(ds, q_ref[:, head]) * scale
+        dq_ref[head, :] = old_ref[head, :] + dot(kv_ref[:, head].T, ds) * scale
+
+
+def grad(queries, dout, kv, p, dp, own, stat, dq):
+    rows, n = kv.shape[0], queries.shape[0]
+    vmem = pl.BlockSpec(memory_space=pltpu.VMEM)
+    return pl.pallas_call(
+        grad_kernel,
+        in_specs=[vmem] * 8,
+        out_specs=[vmem] * 2,
+        out_shape=[
+            jax.ShapeDtypeStruct((W, n), jnp.float32),
+            jax.ShapeDtypeStruct((rows, 2 * W), jnp.float32),
+        ],
+        compiler_params=pltpu.CompilerParams(vmem_limit_bytes=12 * 2**20),
+        cost_estimate=pl.CostEstimate(
+            flops=6 * n * rows * W, bytes_accessed=8 * n * W, transcendentals=0
+        ),
+    )(queries, dout, kv, p, dp, own, stat, dq)
+
+
+def attn_kernel(sizes, groups, early, held, block, *refs):
     q_ref, do_ref, qt_ref, dot_ref = refs[:4]
     pieces = refs[4 : 4 + len(sizes)]
     refs = refs[4 + len(sizes) :]
     scored = {at: refs[3 * e : 3 * e + 3] for e, at in enumerate(early)}
     refs = refs[3 * len(early) :]
     dq_ref = refs[0]
-    outs = refs[1 : 1 + len(groups)]
-    kv_ref, kt_ref, p_ref, dp_ref = refs[1 + len(groups) :]
+    shown = [i for i in range(len(groups)) if i not in held]
+    outs = dict(zip(shown, refs[1:]))
+    refs = refs[1 + len(shown) :]
+    kept = {}
+    for i in held:
+        if i not in scored:
+            kept[i], refs = refs[:2], refs[2:]
+    if held:
+        stat_ref, refs = refs[0], refs[1:]
+    kv_ref, kt_ref, p_ref, dp_ref = refs
     total = sum(sizes)
     scale = 1.0 / math.sqrt(DH)
     to_exp2 = scale * math.log2(math.e)
@@ -76,11 +120,18 @@
     last = pl.num_programs(0) - 1
     spans = [slice(at, at + block) for at in range(0, total, block)]
     places = [
-        (i, outs[i], slice(at, at + block))
+        (i, slice(at, at + block))
         for i, g in enumerate(groups)
         for at in range(0, g, block)
     ]
-    fresh = [span for span, place in zip(spans, places) if place[0] not in scored]
+    fresh = [(span, *place) for span, place in zip(spans, places) if place[0] not in scored]
+
+    def room(h, span, i, part):
+        if i in kept:
+            at = h * groups[i] + part.start
+            return (*kept[i], slice(at, at + block))
+        return (p_ref, dp_ref, span)
+
 
     @pl.when(step == 0)
     def _():
@@ -88,7 +139,7 @@
         for piece, rows in zip(pieces, sizes):
             kv_ref[at : at + rows, :] = piece[...]
             at += rows
-        for out in outs:
+        for out in outs.values():
             out[...] = jnp.zeros_like(out)
         for span in spans:
             kt_ref[:, span] = kv_ref[span, :W].T
@@ -97,9 +148,10 @@
         head = slice(h * DH, (h + 1) * DH)
         vhead = slice(W + h * DH, W + (h + 1) * DH)
         peak = None
-        for span in fresh:
+        for span, i, part in fresh:
+            p_at, dp_at, there = room(h, span, i, part)
             s = dot(kv_ref[span, head], qt_ref[head, :]) * to_exp2
-            p_ref[span, :] = s
+            p_at[there, :] = s
             m = jnp.max(s, axis=0, keepdims=True)
             peak = m if peak is None else jnp.maximum(peak, m)
         for _, _, stat in scored.values():
@@ -111,17 +163,25 @@
             share[i] = jnp.exp2(stat[h : h + 1, :] - peak)
             mass = mass + share[i] * stat[H + h : H + h + 1, :]
             weighted = weighted + share[i] * stat[2 * H + h : 2 * H + h + 1, :]
-        for span in fresh:
+        for span, i, part in fresh:
+            p_at, dp_at, there = room(h, span, i, part)
             dp = dot(kv_ref[span, vhead], dot_ref[head, :])
-            p = jnp.exp2(p_ref[span, :] - peak)
-            p_ref[span, :] = p
-            dp_ref[span, :] = dp
+            p = jnp.exp2(p_at[there, :] - peak)
+            p_at[there, :] = p
+            dp_at[there, :] = dp
             mass = mass + jnp.sum(p, axis=0, keepdims=True)
             weighted = weighted + jnp.sum(p * dp, axis=0, keepdims=True)
         inv = 1.0 / mass
         delta = weighted * inv
+        if held:
+            stat_ref[h : h + 1, :] = peak
+            stat_ref[H + h : H + h + 1, :] = inv
+            stat_ref[2 * H + h : 2 * H + h + 1, :] = delta
         dq = None
-        for span, (i, out, part_rows) in zip(spans, places):
+        for span, (i, part_rows) in zip(spans, places):
+            if i in held:
+                continue
+            out = outs[i]
             if i in scored:
                 at = h * groups[i] + part_rows.start
                 there = slice(at, at + block)
@@ -133,35 +193,40 @@
             ds = (p * (dp - delta)).astype(jnp.bfloat16)
             out[part_rows, vhead] += dot(p.astype(jnp.bfloat16), do_ref[:, head])
             out[part_rows, head] += dot(ds, q_ref[:, head])
-            part = dot(kt_ref[head, span], ds)
-            dq = part if dq is None else dq + part
+            more = dot(kt_ref[head, span], ds)
+            dq = more if dq is None else dq + more
         dq_ref[head, :] = dq * scale
 
     @pl.when(step == last)
     def _():
-        for out in outs:
+        for out in outs.values():
             out[:, :W] = out[:, :W] * scale
 
 
-def attn(queries, dout, queries_t, dout_t, pieces, groups, scored):
+def attn(queries, dout, queries_t, dout_t, pieces, groups, scored, held):
     rows_q = queries.shape[0]
     sizes = [p.shape[0] for p in pieces]
     total = sum(sizes)
     tile = math.gcd(rows_q, 1024 if total <= 1024 else 256)
     block = math.gcd(groups[0], 256)
+    shapes = [(W, rows_q)] + [(g, 2 * W) for i, g in enumerate(groups) if i not in held]
+    for i in held:
+        if i not in scored:
+            shapes += [(H * groups[i], rows_q)] * 2
+    if held:
+        shapes.append((4 * H, rows_q))
     limit = 8 * total * tile + 6 * total * W + 20 * tile * W + 8 * 2**20
     row = pl.BlockSpec((tile, W), lambda i: (i, 0))
     col = pl.BlockSpec((W, tile), lambda i: (0, i))
     vmem = pl.BlockSpec(memory_space=pltpu.VMEM)
     return pl.pallas_call(
-        lambda *refs: attn_kernel(sizes, groups, list(scored), block, *refs),
+        lambda *refs: attn_kernel(sizes, groups, list(scored), held, block, *refs),
         grid=(rows_q // tile,),
         in_specs=[row, row, col, col]
         + [pl.BlockSpec(p.shape, lambda i: (0, 0)) for p in pieces]
         + [vmem] * (3 * len(scored)),
-        out_specs=[col] + [vmem] * len(groups),
-        out_shape=[jax.ShapeDtypeStruct((W, rows_q), jnp.float32)]
-        + [jax.ShapeDtypeStruct((g, 2 * W), jnp.float32) for g in groups],
+        out_specs=[col] + [vmem] * (len(shapes) - 1),
+        out_shape=[jax.ShapeDtypeStruct(shape, jnp.float32) for shape in shapes],
         scratch_shapes=[
             pltpu.VMEM((total, 2 * W), jnp.bfloat16),
             pltpu.VMEM((W, total), jnp.bfloat16),
@@ -205,11 +270,21 @@
     if early:
         late, _ = lax.optimization_barrier((near_o, far_all))
         scored[1] = score(queries_t, dout_t, late)
-    dq, g_far_o, g_near_o, g_far, g_near = attn(
-        queries, dout, queries_t, dout_t, [far_o, near_o, far_all, near], [many] * 4, scored
-    )
-    g_far_o = swap(g_far_o, "pb", 1)
-    g_near_o = swap(g_near_o, "pb", 1)
+    pieces, groups = [far_o, near_o, far_all, near], [many] * 4
+    if early:
+        dq, g_far_o, g_near_o, p, dp, stat = attn(
+            queries, dout, queries_t, dout_t, pieces, groups, scored, [2, 3]
+        )
+        g_far_o = swap(g_far_o, "pb", 1)
+        g_near_o = swap(g_near_o, "pb", 1)
+        dq, g_far = grad(queries, dout, far_all, p, dp, stat, stat, dq)
+        dq, g_near = grad(queries, dout, near, *scored[3], stat, dq)
+    else:
+        dq, g_far_o, g_near_o, g_far, g_near = attn(
+            queries, dout, queries_t, dout_t, pieces, groups, scored, []
+        )
+        g_far_o = swap(g_far_o, "pb", 1)
+        g_near_o = swap(g_near_o, "pb", 1)
 
     def rows(x, k):
         return x[k * half : (k + 1) * half]
@@ -218,9 +293,9 @@
         sent = (rows(g_far, k) + rows(g_far_o, k)).astype(jnp.bfloat16)
         return swap(sent, "kv", 1)
 
-    arrived = {k: from_far(k) for k in range(1, lines)}
-    g_far, _ = lax.optimization_barrier((g_far, arrived[1]))
-    arrived[0] = from_far(0)
+    arrived = {}
+    for k in list(range(1, lines)) + [0]:
+        arrived[k] = from_far(k)
 
     def merged(k):
         return rows(g_near, k) + rows(g_near_o, k) + arrived[k].astype(jnp.float32)

time: 53.7 us -> 51.5 us (0.959)
  starting transfers between devices: 22.4 us -> 19.9 us
    ppermute x6, starting transfers between devices: 11.2 us -> 9.2 us  [shift(): return lax.ppermute(x, axis, [(i, (i + by) % n) for i in range(n)])]
    ppermute x14, waiting for transfers between devices: 9.49 us -> 10.3 us  [swap(): return lax.ppermute(x, axis, [(i, i ^ bit) for i in range(n)])]
    ppermute x6, waiting for transfers between devices: 7.85 us -> 7.29 us  [shift(): return lax.ppermute(x, axis, [(i, (i + by) % n) for i in range(n)])]
    pallas_call x1 -> x3, Pallas kernels: 5.57 us -> 5.55 us  [the longest x1 3.84 us: attn(): pl.pallas_call(lambda *refs: attn_kernel(sizes, groups, list(scored), hel...]
  transfers between devices with their start and end apart: 20 -> 20, of which waited for: 9 -> 9; matrix products, arithmetic and copies ran while one was open for 7% -> 8% of each run, Pallas kernels for 3% -> 7%
where the time goes in v1:
time: 51.5 us; the launch traced here: 51.2 us
  starting transfers between devices  19.9 us (39%)
  waiting for transfers between devices  17.6 us (34%)
  Pallas kernels  7.26 us (14%)
  local copies, waits for them, and re-layouts  3.84 us (7%)
  other arithmetic  1.8 us (3%)
  between operations  0.83 us (2%)
    ppermute x14, starting transfers between devices, swap(): return lax.ppermute(x, axis, [(i, i ^ bit) for i in range(n)])  10.7 us
    ppermute x14, waiting for transfers between devices, swap(): return lax.ppermute(x, axis, [(i, i ^ bit) for i in range(n)])  10.3 us
    ppermute x6, starting transfers between devices, shift(): return lax.ppermute(x, axis, [(i, (i + by) % n) for i in range(n)])  9.2 us
    ppermute x6, waiting for transfers between devices, shift(): return lax.ppermute(x, axis, [(i, (i + by) % n) for i in range(n)])  7.29 us
    pallas_call x1, Pallas kernels, attn(): pl.pallas_call(lambda *refs: attn_kernel(sizes, groups, list(scored), hel...  3.84 us
    unnamed x10, local copies, waits for them, and re-layouts  3.83 us
    pallas_call x2, Pallas kernels, grad(): pl.pallas_call(grad_kernel, in_specs=[vmem] * 8, out_specs=[vmem] * 2, ou...  1.71 us
    pallas_call x2, Pallas kernels, score(): pl.pallas_call(lambda *refs: score_kernel(math.log2(math.e) / math.sqrt(D...  1.71 us
  transfers between devices with their start and end apart: 20, of which 9 were waited for; matrix products, arithmetic and copies ran while one was open for 8% of the time, Pallas kernels for 7%

profile of v1, /device:TPU:0, one launch (start us, length us, event | category | flops | bytes accessed | tf_op | source)
XLA Modules:
  0.0 51.2 jit_solution(12142857016438305205)
XLA Ops:
  0.6 0.8 %fusion.15 = bf16[64,512]{1,0:T(8,128)(2,1)S(1)} fusion(s32[]{:T(128)S(6)} %select_n.23, bf16[128,256]{1,0:T(8,128)(2,1)} %param.5, bf16[128,256]{1,0:T(8,128)(2,1)} %param.6), kind=kLoop, calls=%fused_computation.29 | loop fusion | flops 131072 | bytes 196612 | tf_op jit(solution)/shard_map/concatenate | solution.py:251
  1.4 5.1 %collective-permute-start.2 = (bf16[64,512]{1,0:T(8,128)(2,1)S(1)}, bf16[64,512]{1,0:T(8,128)(2,1)S(1)}, u32[]{:S(2)}, u32[]{:S(2)}) collective-permute-start(bf16[64,512]{1,0:T(8,128)(2,1)S(1)} %fusion.15), channel_id=1, source_target_pairs={{0,6},{1,7},{2,0},{3,1},{4,2},{5,3},{6,4},{7,5},{8,14},{9,15},{10,... | collective-permute-start | bytes 196616 | tf_op jit(solution)/shard_map/ppermute | solution.py:23
  6.5 0.0 collective-permute-start.1
  6.5 1.0 %collective-permute-start = (bf16[64,512]{1,0:T(8,128)(2,1)S(1)}, bf16[64,512]{1,0:T(8,128)(2,1)S(1)}, u32[]{:S(2)}, u32[]{:S(2)}) collective-permute-start(bf16[64,512]{1,0:T(8,128)(2,1)S(1)} %fusion.15), channel_id=1, source_target_pairs={{0,4},{1,5},{2,6},{3,7},{4,0},{5,1},{6,2},{7,3},{8,12},{9,13},{10,... | collective-permute-start | bytes 196616 | tf_op jit(solution)/shard_map/ppermute | solution.py:23
  7.5 1.5 %collective-permute-start.3 = (bf16[64,512]{1,0:T(8,128)(2,1)S(1)}, bf16[64,512]{1,0:T(8,128)(2,1)S(1)}, u32[]{:S(2)}, u32[]{:S(2)}) collective-permute-start(bf16[64,512]{1,0:T(8,128)(2,1)S(1)} %fusion.15), channel_id=1, source_target_pairs={{0,1},{1,0},{2,3},{3,2},{4,5},{5,4},{6,7},{7,6},{8,9},{9,8},{10,11... | collective-permute-start | bytes 196616 | tf_op jit(solution)/shard_map/ppermute | solution.py:18
  9.0 1.2 %copy.7 = bf16[1024,256]{0,1:T(8,128)(2,1)S(1)} copy(bf16[1024,256]{1,0:T(8,128)(2,1)} %refs_0_.5) | data formatting | bytes 1048576 | tf_op args[0]
  10.3 1.2 %copy.8 = bf16[1024,256]{0,1:T(8,128)(2,1)S(1)} copy(bf16[1024,256]{1,0:T(8,128)(2,1)} %refs_1_.5) | data formatting | bytes 1048576 | tf_op args[3]
  11.5 0.0 copy-start
  11.6 0.0 copy-start.1
  11.6 0.0 collective-permute-done.2
  11.6 0.6 %collective-permute-start.6 = (bf16[64,512]{1,0:T(8,128)(2,1)S(1)}, bf16[64,512]{1,0:T(8,128)(2,1)S(1)}, u32[]{:S(2)}, u32[]{:S(2)}) collective-permute-start(bf16[64,512]{1,0:T(8,128)(2,1)S(1)} %collective-permute-done.2), channel_id=1, source_target_pairs={{0,1},{1,0},{2,3},{3,2},{4,5},{5,4},{6,7},{7,6},{8,9},{9,8},{10,11... | collective-permute-start | bytes 196616 | tf_op jit(solution)/shard_map/ppermute | solution.py:18
  12.2 0.5 collective-permute-done.1
  12.7 1.3 %collective-permute-done = bf16[64,512]{1,0:T(8,128)(2,1)S(1)} collective-permute-done((bf16[64,512]{1,0:T(8,128)(2,1)S(1)}, bf16[64,512]{1,0:T(8,128)(2,1)S(1)}, u32[]{:S(2)}, u32[]{:S(2)}) %collective-permute-start) | collective-permute-done | bytes 65568 | tf_op jit(solution)/shard_map/ppermute | solution.py:23
  14.0 0.1 collective-permute-start.8
  14.1 1.6 %collective-permute-start.5 = (bf16[64,512]{1,0:T(8,128)(2,1)S(1)}, bf16[64,512]{1,0:T(8,128)(2,1)S(1)}, u32[]{:S(2)}, u32[]{:S(2)}) collective-permute-start(bf16[64,512]{1,0:T(8,128)(2,1)S(1)} %collective-permute-done.1), channel_id=1, source_target_pairs={{0,1},{1,0},{2,3},{3,2},{4,5},{5,4},{6,7},{7,6},{8,9},{9,8},{10,11... | collective-permute-start | bytes 196616 | tf_op jit(solution)/shard_map/ppermute | solution.py:18
  15.7 0.5 collective-permute-start.4
  16.2 0.0 collective-permute-done.3
  16.2 0.9 %shard_map.67 = (f32[512,1024]{1,0:T(8,128)S(1)}, f32[512,1024]{1,0:T(8,128)S(1)}, f32[8,1024]{1,0:T(8,128)S(1)}) custom-call(bf16[256,1024]{1,0:T(8,128)(2,1)S(1)} %bitcast.3, bf16[256,1024]{1,0:T(8,128)(2,1)S(1)} %bitcast.6, bf16[256,512]{1,0:T(8,128)(2,1)S(1)} %pad_maximum_fusion.refs_2_.refs_7_), custom_call_target="tpu_custom_call" | custom-call | flops 268435456 | bytes 2097152 | tf_op jit(solution)/shard_map/pallas_call | solution.py:51
  17.0 0.0 collective-permute-done.6
  17.0 2.9 %collective-permute-done.4 = bf16[64,512]{1,0:T(8,128)(2,1)S(1)} collective-permute-done((bf16[64,512]{1,0:T(8,128)(2,1)S(1)}, bf16[64,512]{1,0:T(8,128)(2,1)S(1)}, u32[]{:S(2)}, u32[]{:S(2)}) %collective-permute-start.4) | collective-permute-done | bytes 65568 | tf_op jit(solution)/shard_map/ppermute | solution.py:18
  20.0 0.0 collective-permute-done.5
  20.0 0.1 collective-permute-start.7
  20.1 0.9 %shard_map.68 = (f32[512,1024]{1,0:T(8,128)S(1)}, f32[512,1024]{1,0:T(8,128)S(1)}, f32[8,1024]{1,0:T(8,128)S(1)}) custom-call(bf16[256,1024]{1,0:T(8,128)(2,1)S(1)} %bitcast.4, bf16[256,1024]{1,0:T(8,128)(2,1)S(1)} %bitcast.7, bf16[256,512]{1,0:T(8,128)(2,1)S(1)} %collective-permute-done.8.refs_2_.refs_5_), custom_call_target="tpu_custom_call" | custom-call | flops 268435456 | bytes 2097152 | tf_op jit(solution)/shard_map/pallas_call | solution.py:51
  21.0 0.7 %collective-permute-done.7.refs_4_ = bf16[256,512]{1,0:T(8,128)(2,1)S(1)} collective-permute-done((bf16[256,512]{1,0:T(8,128)(2,1)S(1)}, bf16[256,512]{1,0:T(8,128)(2,1)S(1)}, u32[]{:S(2)}, u32[]{:S(2)}) %collective-permute-start.7) | collective-permute-done | bytes 262176 | tf_op jit(solution)/shard_map/ppermute | solution.py:18
  21.6 3.8 %shard_map.69 = (f32[256,1024]{1,0:T(8,128)S(1)}, f32[256,512]{1,0:T(8,128)S(1)}, f32[256,512]{1,0:T(8,128)S(1)}, f32[512,1024]{1,0:T(8,128)S(1)}, f32[512,1024]{1,0:T(8,128)S(1)}, /*index=5*/f32[8,1024]{1,0:T(8,128)S(1)}) custom-call(bf16[1024,256]{1,0:T(8,128)(2,1)S(1)} %copy-done, bf16[1024,256]{1,0:T(8,128)(2,1)S(1)} %copy-done.1, ...), custom_call_target="tpu_custom_call" | custom-call | flops 2684354560 | bytes 2097152 | tf_op jit(solution)/shard_map/pallas_call | solution.py:222
  25.5 0.2 collective-permute-start.10
  25.7 0.4 collective-permute-start.9
  26.0 0.9 %shard_map.70 = (f32[256,1024]{1,0:T(8,128)S(1)}, f32[256,512]{1,0:T(8,128)S(1)}) custom-call(bf16[1024,256]{1,0:T(8,128)(2,1)S(1)} %copy-done, bf16[1024,256]{1,0:T(8,128)(2,1)S(1)} %copy-done.1, bf16[256,512]{1,0:T(8,128)(2,1)S(1)} %constant_dynamic-update-slice_fusion.refs_6_.refs_2_, f32[512,1024]{1,0:T(8,128)S(1)} %get-tuple-element.39.refs_3_, ...), custom_call_target="tpu_custom_call" | custom-call | flops 402653184 | bytes 2097152 | tf_op jit(solution)/shard_map/pallas_call | solution.py:84
  26.9 0.5 %collective-permute-done.10 = f32[256,512]{1,0:T(8,128)S(1)} collective-permute-done((f32[256,512]{1,0:T(8,128)S(1)}, f32[256,512]{1,0:T(8,128)S(1)}, u32[]{:S(2)}, u32[]{:S(2)}) %collective-permute-start.10) | collective-permute-done | bytes 524320 | tf_op jit(solution)/shard_map/ppermute | solution.py:18
  27.4 0.1 fusion.10
  27.5 1.6 %collective-permute-start.14 = (bf16[64,512]{1,0:T(8,128)(2,1)S(1)}, bf16[64,512]{1,0:T(8,128)(2,1)S(1)}, u32[]{:S(2)}, u32[]{:S(2)}) collective-permute-start(bf16[64,512]{1,0:T(8,128)(2,1)S(1)} %get-tuple-element.55), channel_id=1, source_target_pairs={{0,1},{1,0},{2,3},{3,2},{4,5},{5,4},{6,7},{7,6},{8,9},{9,8},{10,11... | collective-permute-start | bytes 196616 | tf_op jit(solution)/shard_map/ppermute | solution.py:18
  29.1 0.9 %shard_map.71 = (f32[256,1024]{1,0:T(8,128)S(1)}, f32[256,512]{1,0:T(8,128)S(1)}) custom-call(bf16[1024,256]{1,0:T(8,128)(2,1)S(1)} %copy-done, bf16[1024,256]{1,0:T(8,128)(2,1)S(1)} %copy-done.1, bf16[256,512]{1,0:T(8,128)(2,1)S(1)} %pad_maximum_fusion.refs_2_.refs_7_, f32[512,1024]{1,0:T(8,128)S(1)} %get-tuple-element.30.refs_8_.refs_3_, ...), custom_call_target="tpu_custom_call" | custom-call | flops 402653184 | bytes 2097152 | tf_op jit(solution)/shard_map/pallas_call | solution.py:84
  30.0 0.6 %collective-permute-start.11 = (bf16[64,512]{1,0:T(8,128)(2,1)S(1)}, bf16[64,512]{1,0:T(8,128)(2,1)S(1)}, u32[]{:S(2)}, u32[]{:S(2)}) collective-permute-start(bf16[64,512]{1,0:T(8,128)(2,1)S(1)} %get-tuple-element.54), channel_id=1, source_target_pairs={{0,1},{1,0},{2,3},{3,2},{4,5},{5,4},{6,7},{7,6},{8,9},{9,8},{10,11... | collective-permute-start | bytes 196616 | tf_op jit(solution)/shard_map/ppermute | solution.py:18
  30.6 1.5 %collective-permute-start.13 = (bf16[64,512]{1,0:T(8,128)(2,1)S(1)}, bf16[64,512]{1,0:T(8,128)(2,1)S(1)}, u32[]{:S(2)}, u32[]{:S(2)}) collective-permute-start(bf16[64,512]{1,0:T(8,128)(2,1)S(1)} %get-tuple-element.56), channel_id=1, source_target_pairs={{0,1},{1,0},{2,3},{3,2},{4,5},{5,4},{6,7},{7,6},{8,9},{9,8},{10,11... | collective-permute-start | bytes 196616 | tf_op jit(solution)/shard_map/ppermute | solution.py:18
  32.1 0.5 collective-permute-start.12
  32.6 0.7 %collective-permute-start.15 = (bf16[64,512]{1,0:T(8,128)(2,1)S(1)}, bf16[64,512]{1,0:T(8,128)(2,1)S(1)}, u32[]{:S(2)}, u32[]{:S(2)}) collective-permute-start(bf16[64,512]{1,0:T(8,128)(2,1)S(1)} %fusion.3), channel_id=1, source_target_pairs={{0,4},{1,5},{2,6},{3,7},{4,0},{5,1},{6,2},{7,3},{8,12},{9,13},{10,... | collective-permute-start | bytes 196616 | tf_op jit(solution)/shard_map/ppermute | solution.py:23
  33.4 2.7 %collective-permute-done.13 = bf16[64,512]{1,0:T(8,128)(2,1)S(1)} collective-permute-done((bf16[64,512]{1,0:T(8,128)(2,1)S(1)}, bf16[64,512]{1,0:T(8,128)(2,1)S(1)}, u32[]{:S(2)}, u32[]{:S(2)}) %collective-permute-start.13) | collective-permute-done | bytes 65568 | tf_op jit(solution)/shard_map/ppermute | solution.py:18
  36.1 1.7 %collective-permute-start.16 = (bf16[64,512]{1,0:T(8,128)(2,1)S(1)}, bf16[64,512]{1,0:T(8,128)(2,1)S(1)}, u32[]{:S(2)}, u32[]{:S(2)}) collective-permute-start(bf16[64,512]{1,0:T(8,128)(2,1)S(1)} %fusion.6), channel_id=1, source_target_pairs={{0,6},{1,7},{2,0},{3,1},{4,2},{5,3},{6,4},{7,5},{8,14},{9,15},{10,... | collective-permute-start | bytes 196616 | tf_op jit(solution)/shard_map/ppermute | solution.py:23
  37.8 0.6 %collective-permute-start.17 = (bf16[64,512]{1,0:T(8,128)(2,1)S(1)}, bf16[64,512]{1,0:T(8,128)(2,1)S(1)}, u32[]{:S(2)}, u32[]{:S(2)}) collective-permute-start(bf16[64,512]{1,0:T(8,128)(2,1)S(1)} %fusion.9), channel_id=1, source_target_pairs={{0,2},{1,3},{2,4},{3,5},{4,6},{5,7},{6,0},{7,1},{8,10},{9,11},{10,... | collective-permute-start | bytes 196616 | tf_op jit(solution)/shard_map/ppermute | solution.py:23
  38.5 1.9 %collective-permute-done.16 = bf16[64,512]{1,0:T(8,128)(2,1)S(1)} collective-permute-done((bf16[64,512]{1,0:T(8,128)(2,1)S(1)}, bf16[64,512]{1,0:T(8,128)(2,1)S(1)}, u32[]{:S(2)}, u32[]{:S(2)}) %collective-permute-start.16) | collective-permute-done | bytes 65568 | tf_op jit(solution)/shard_map/ppermute | solution.py:23
  40.4 3.6 %collective-permute-done.17 = bf16[64,512]{1,0:T(8,128)(2,1)S(1)} collective-permute-done((bf16[64,512]{1,0:T(8,128)(2,1)S(1)}, bf16[64,512]{1,0:T(8,128)(2,1)S(1)}, u32[]{:S(2)}, u32[]{:S(2)}) %collective-permute-start.17) | collective-permute-done | bytes 65568 | tf_op jit(solution)/shard_map/ppermute | solution.py:23
  43.9 0.1 fusion.14
  44.0 1.6 %collective-permute-start.18 = (f32[64,512]{1,0:T(8,128)S(1)}, f32[64,512]{1,0:T(8,128)S(1)}, u32[]{:S(2)}, u32[]{:S(2)}) collective-permute-start(f32[64,512]{1,0:T(8,128)S(1)} %fusion.14), channel_id=1, source_target_pairs={{0,16},{8,24},{16,0},{24,8},{1,17},{9,25},{17,1},{25,9},{2,18},{10... | collective-permute-start | bytes 393224 | tf_op jit(solution)/shard_map/ppermute | solution.py:18
  45.6 3.5 %collective-permute-done.18 = f32[64,512]{1,0:T(8,128)S(1)} collective-permute-done((f32[64,512]{1,0:T(8,128)S(1)}, f32[64,512]{1,0:T(8,128)S(1)}, u32[]{:S(2)}, u32[]{:S(2)}) %collective-permute-start.18) | collective-permute-done | bytes 131104 | tf_op jit(solution)/shard_map/ppermute | solution.py:18
  49.0 0.1 collective-permute-start.19
  49.1 1.3 %copy.9 = f32[1024,256]{1,0:T(8,128)} copy(f32[1024,256]{0,1:T(8,128)S(1)} %bitcast.9) | data formatting | bytes 2097152
  50.4 0.0 collective-permute-done.19
  50.5 0.7 %pad_maximum_fusion.1 = (f32[128,256]{1,0:T(8,128)}, f32[128,256]{1,0:T(8,128)}) fusion(f32[64,512]{1,0:T(8,128)S(1)} %get-tuple-element.60, f32[64,512]{1,0:T(8,128)S(1)} %get-tuple-element.61), kind=kLoop, calls=%fused_computation.4 | loop fusion | flops 65536 | bytes 524288 | tf_op jit(solution)/shard_map/concatenate | solution.py:317
  (18 shorter events, 0.2 us)
Async XLA Ops:
  1.4 10.1 %collective-permute-start.2 = (bf16[64,512]{1,0:T(8,128)(2,1)S(1)}, bf16[64,512]{1,0:T(8,128)(2,1)S(1)}, u32[]{:S(2)}, u32[]{:S(2)}) collective-permute-start(bf16[64,512]{1,0:T(8,128)(2,1)S(1)} %fusion.15), channel_id=1, source_target_pairs={{0,6},{1,7},{2,0},{3,1},{4,2},{5,3},{6,4},{7,5},{8,14},{9,15},{10,... | collective-permute-start | bytes 196616 | tf_op jit(solution)/shard_map/ppermute | solution.py:23
  6.5 6.2 %collective-permute-start.1 = (bf16[64,512]{1,0:T(8,128)(2,1)S(1)}, bf16[64,512]{1,0:T(8,128)(2,1)S(1)}, u32[]{:S(2)}, u32[]{:S(2)}) collective-permute-start(bf16[64,512]{1,0:T(8,128)(2,1)S(1)} %fusion.15), channel_id=1, source_target_pairs={{0,2},{1,3},{2,4},{3,5},{4,6},{5,7},{6,0},{7,1},{8,10},{9,11},{10,... | collective-permute-start | bytes 196616 | tf_op jit(solution)/shard_map/ppermute | solution.py:23
  6.5 7.5 %collective-permute-start = (bf16[64,512]{1,0:T(8,128)(2,1)S(1)}, bf16[64,512]{1,0:T(8,128)(2,1)S(1)}, u32[]{:S(2)}, u32[]{:S(2)}) collective-permute-start(bf16[64,512]{1,0:T(8,128)(2,1)S(1)} %fusion.15), channel_id=1, source_target_pairs={{0,4},{1,5},{2,6},{3,7},{4,0},{5,1},{6,2},{7,3},{8,12},{9,13},{10,... | collective-permute-start | bytes 196616 | tf_op jit(solution)/shard_map/ppermute | solution.py:23
  7.5 8.6 %collective-permute-start.3 = (bf16[64,512]{1,0:T(8,128)(2,1)S(1)}, bf16[64,512]{1,0:T(8,128)(2,1)S(1)}, u32[]{:S(2)}, u32[]{:S(2)}) collective-permute-start(bf16[64,512]{1,0:T(8,128)(2,1)S(1)} %fusion.15), channel_id=1, source_target_pairs={{0,1},{1,0},{2,3},{3,2},{4,5},{5,4},{6,7},{7,6},{8,9},{9,8},{10,11... | collective-permute-start | bytes 196616 | tf_op jit(solution)/shard_map/ppermute | solution.py:18
  11.5 10.1 %copy-start = (bf16[1024,256]{1,0:T(8,128)(2,1)S(1)}, bf16[1024,256]{1,0:T(8,128)(2,1)}, u32[]{:S(2)}) copy-start(bf16[1024,256]{1,0:T(8,128)(2,1)} %refs_0_.5) | copy-start | bytes 1572868
  11.6 10.1 %copy-start.1 = (bf16[1024,256]{1,0:T(8,128)(2,1)S(1)}, bf16[1024,256]{1,0:T(8,128)(2,1)}, u32[]{:S(2)}) copy-start(bf16[1024,256]{1,0:T(8,128)(2,1)} %refs_1_.5) | copy-start | bytes 1572868
  11.6 5.5 %collective-permute-start.6 = (bf16[64,512]{1,0:T(8,128)(2,1)S(1)}, bf16[64,512]{1,0:T(8,128)(2,1)S(1)}, u32[]{:S(2)}, u32[]{:S(2)}) collective-permute-start(bf16[64,512]{1,0:T(8,128)(2,1)S(1)} %collective-permute-done.2), channel_id=1, source_target_pairs={{0,1},{1,0},{2,3},{3,2},{4,5},{5,4},{6,7},{7,6},{8,9},{9,8},{10,11... | collective-permute-start | bytes 196616 | tf_op jit(solution)/shard_map/ppermute | solution.py:18
  14.0 6.1 %collective-permute-start.8 = (bf16[256,512]{1,0:T(8,128)(2,1)S(1)}, bf16[256,512]{1,0:T(8,128)(2,1)S(1)}, u32[]{:S(2)}, u32[]{:S(2)}) collective-permute-start(bf16[256,512]{1,0:T(8,128)(2,1)S(1)} %pad_maximum_fusion.refs_2_.refs_7_), channel_id=1, source_target_pairs={{0,8},{8,0},{16,24},{24,16},{1,9},{9,1},{17,25},{25,17},{2,10},{10... | collective-permute-start | bytes 786440 | tf_op jit(solution)/shard_map/ppermute | solution.py:18
  14.1 5.9 %collective-permute-start.5 = (bf16[64,512]{1,0:T(8,128)(2,1)S(1)}, bf16[64,512]{1,0:T(8,128)(2,1)S(1)}, u32[]{:S(2)}, u32[]{:S(2)}) collective-permute-start(bf16[64,512]{1,0:T(8,128)(2,1)S(1)} %collective-permute-done.1), channel_id=1, source_target_pairs={{0,1},{1,0},{2,3},{3,2},{4,5},{5,4},{6,7},{7,6},{8,9},{9,8},{10,11... | collective-permute-start | bytes 196616 | tf_op jit(solution)/shard_map/ppermute | solution.py:18
  15.7 4.3 %collective-permute-start.4 = (bf16[64,512]{1,0:T(8,128)(2,1)S(1)}, bf16[64,512]{1,0:T(8,128)(2,1)S(1)}, u32[]{:S(2)}, u32[]{:S(2)}) collective-permute-start(bf16[64,512]{1,0:T(8,128)(2,1)S(1)} %collective-permute-done), channel_id=1, source_target_pairs={{0,1},{1,0},{2,3},{3,2},{4,5},{5,4},{6,7},{7,6},{8,9},{9,8},{10,11... | collective-permute-start | bytes 196616 | tf_op jit(solution)/shard_map/ppermute | solution.py:18
  20.0 1.6 %collective-permute-start.7 = (bf16[256,512]{1,0:T(8,128)(2,1)S(1)}, bf16[256,512]{1,0:T(8,128)(2,1)S(1)}, u32[]{:S(2)}, u32[]{:S(2)}) collective-permute-start(bf16[256,512]{1,0:T(8,128)(2,1)S(1)} %constant_dynamic-update-slice_fusion.refs_6_.refs_2_), channel_id=1, source_target_pairs={{0,8},{8,0},{16,24},{24,16},{1,9},{9,1},{17,25},{25,17},{2,10},{10... | collective-permute-start | bytes 786440 | tf_op jit(solution)/shard_map/ppermute | solution.py:18
  25.5 2.0 %collective-permute-start.10 = (f32[256,512]{1,0:T(8,128)S(1)}, f32[256,512]{1,0:T(8,128)S(1)}, u32[]{:S(2)}, u32[]{:S(2)}) collective-permute-start(f32[256,512]{1,0:T(8,128)S(1)} %get-tuple-element.47), channel_id=1, source_target_pairs={{0,8},{8,0},{16,24},{24,16},{1,9},{9,1},{17,25},{25,17},{2,10},{10... | collective-permute-start | bytes 1572872 | tf_op jit(solution)/shard_map/ppermute | solution.py:18
  25.7 6.9 %collective-permute-start.9 = (f32[256,512]{1,0:T(8,128)S(1)}, f32[256,512]{1,0:T(8,128)S(1)}, u32[]{:S(2)}, u32[]{:S(2)}) collective-permute-start(f32[256,512]{1,0:T(8,128)S(1)} %get-tuple-element.45), channel_id=1, source_target_pairs={{0,8},{8,0},{16,24},{24,16},{1,9},{9,1},{17,25},{25,17},{2,10},{10... | collective-permute-start | bytes 1572872 | tf_op jit(solution)/shard_map/ppermute | solution.py:18
  27.5 5.1 %collective-permute-start.14 = (bf16[64,512]{1,0:T(8,128)(2,1)S(1)}, bf16[64,512]{1,0:T(8,128)(2,1)S(1)}, u32[]{:S(2)}, u32[]{:S(2)}) collective-permute-start(bf16[64,512]{1,0:T(8,128)(2,1)S(1)} %get-tuple-element.55), channel_id=1, source_target_pairs={{0,1},{1,0},{2,3},{3,2},{4,5},{5,4},{6,7},{7,6},{8,9},{9,8},{10,11... | collective-permute-start | bytes 196616 | tf_op jit(solution)/shard_map/ppermute | solution.py:18
  30.0 8.5 %collective-permute-start.11 = (bf16[64,512]{1,0:T(8,128)(2,1)S(1)}, bf16[64,512]{1,0:T(8,128)(2,1)S(1)}, u32[]{:S(2)}, u32[]{:S(2)}) collective-permute-start(bf16[64,512]{1,0:T(8,128)(2,1)S(1)} %get-tuple-element.54), channel_id=1, source_target_pairs={{0,1},{1,0},{2,3},{3,2},{4,5},{5,4},{6,7},{7,6},{8,9},{9,8},{10,11... | collective-permute-start | bytes 196616 | tf_op jit(solution)/shard_map/ppermute | solution.py:18
  30.6 5.5 %collective-permute-start.13 = (bf16[64,512]{1,0:T(8,128)(2,1)S(1)}, bf16[64,512]{1,0:T(8,128)(2,1)S(1)}, u32[]{:S(2)}, u32[]{:S(2)}) collective-permute-start(bf16[64,512]{1,0:T(8,128)(2,1)S(1)} %get-tuple-element.56), channel_id=1, source_target_pairs={{0,1},{1,0},{2,3},{3,2},{4,5},{5,4},{6,7},{7,6},{8,9},{9,8},{10,11... | collective-permute-start | bytes 196616 | tf_op jit(solution)/shard_map/ppermute | solution.py:18
  32.1 5.7 %collective-permute-start.12 = (bf16[64,512]{1,0:T(8,128)(2,1)S(1)}, bf16[64,512]{1,0:T(8,128)(2,1)S(1)}, u32[]{:S(2)}, u32[]{:S(2)}) collective-permute-start(bf16[64,512]{1,0:T(8,128)(2,1)S(1)} %get-tuple-element.57), channel_id=1, source_target_pairs={{0,1},{1,0},{2,3},{3,2},{4,5},{5,4},{6,7},{7,6},{8,9},{9,8},{10,11... | collective-permute-start | bytes 196616 | tf_op jit(solution)/shard_map/ppermute | solution.py:18
  32.6 5.8 %collective-permute-start.15 = (bf16[64,512]{1,0:T(8,128)(2,1)S(1)}, bf16[64,512]{1,0:T(8,128)(2,1)S(1)}, u32[]{:S(2)}, u32[]{:S(2)}) collective-permute-start(bf16[64,512]{1,0:T(8,128)(2,1)S(1)} %fusion.3), channel_id=1, source_target_pairs={{0,4},{1,5},{2,6},{3,7},{4,0},{5,1},{6,2},{7,3},{8,12},{9,13},{10,... | collective-permute-start | bytes 196616 | tf_op jit(solution)/shard_map/ppermute | solution.py:23
  36.1 4.3 %collective-permute-start.16 = (bf16[64,512]{1,0:T(8,128)(2,1)S(1)}, bf16[64,512]{1,0:T(8,128)(2,1)S(1)}, u32[]{:S(2)}, u32[]{:S(2)}) collective-permute-start(bf16[64,512]{1,0:T(8,128)(2,1)S(1)} %fusion.6), channel_id=1, source_target_pairs={{0,6},{1,7},{2,0},{3,1},{4,2},{5,3},{6,4},{7,5},{8,14},{9,15},{10,... | collective-permute-start | bytes 196616 | tf_op jit(solution)/shard_map/ppermute | solution.py:23
  37.8 6.1 %collective-permute-start.17 = (bf16[64,512]{1,0:T(8,128)(2,1)S(1)}, bf16[64,512]{1,0:T(8,128)(2,1)S(1)}, u32[]{:S(2)}, u32[]{:S(2)}) collective-permute-start(bf16[64,512]{1,0:T(8,128)(2,1)S(1)} %fusion.9), channel_id=1, source_target_pairs={{0,2},{1,3},{2,4},{3,5},{4,6},{5,7},{6,0},{7,1},{8,10},{9,11},{10,... | collective-permute-start | bytes 196616 | tf_op jit(solution)/shard_map/ppermute | solution.py:23
  44.0 5.0 %collective-permute-start.18 = (f32[64,512]{1,0:T(8,128)S(1)}, f32[64,512]{1,0:T(8,128)S(1)}, u32[]{:S(2)}, u32[]{:S(2)}) collective-permute-start(f32[64,512]{1,0:T(8,128)S(1)} %fusion.14), channel_id=1, source_target_pairs={{0,16},{8,24},{16,0},{24,8},{1,17},{9,25},{17,1},{25,9},{2,18},{10... | collective-permute-start | bytes 393224 | tf_op jit(solution)/shard_map/ppermute | solution.py:18
  49.0 1.4 %collective-permute-start.19 = (f32[64,512]{1,0:T(8,128)S(1)}, f32[64,512]{1,0:T(8,128)S(1)}, u32[]{:S(2)}, u32[]{:S(2)}) collective-permute-start(f32[64,512]{1,0:T(8,128)S(1)} %add.72), channel_id=1, source_target_pairs={{0,8},{8,0},{16,24},{24,16},{1,9},{9,1},{17,25},{25,17},{2,10},{10... | collective-permute-start | bytes 393224 | tf_op jit(solution)/shard_map/ppermute | solution.py:18

commit v2 on v1

--- a/solution.py
+++ b/solution.py
@@ -263,21 +263,21 @@
     early = 4 * many <= queries.shape[0]
     if early:
         scored[3] = score(queries_t, dout_t, near)
-        far[-1], _ = lax.optimization_barrier((far[-1], scored[3][2]))
+        scored[1] = score(queries_t, dout_t, near_o)
+        far, _ = lax.optimization_barrier((far, (scored[1][2], scored[3][2])))
     far_all = jnp.concatenate(far, axis=0)
     far_o = swap(far_all, "pb", 1)
 
     if early:
-        late, _ = lax.optimization_barrier((near_o, far_all))
-        scored[1] = score(queries_t, dout_t, late)
+        scored[2] = score(queries_t, dout_t, far_all)
     pieces, groups = [far_o, near_o, far_all, near], [many] * 4
     if early:
-        dq, g_far_o, g_near_o, p, dp, stat = attn(
+        dq, g_far_o, g_near_o, stat = attn(
             queries, dout, queries_t, dout_t, pieces, groups, scored, [2, 3]
         )
         g_far_o = swap(g_far_o, "pb", 1)
         g_near_o = swap(g_near_o, "pb", 1)
-        dq, g_far = grad(queries, dout, far_all, p, dp, stat, stat, dq)
+        dq, g_far = grad(queries, dout, far_all, *scored[2], stat, dq)
         dq, g_near = grad(queries, dout, near, *scored[3], stat, dq)
     else:
         dq, g_far_o, g_near_o, g_far, g_near = attn(
@@ -294,17 +294,18 @@
         return swap(sent, "kv", 1)
 
     arrived = {}
-    for k in list(range(1, lines)) + [0]:
+    sends = list(range(lines - 1, 0, -1))
+    for k in sends + [0]:
         arrived[k] = from_far(k)
 
     def merged(k):
         return rows(g_near, k) + rows(g_near_o, k) + arrived[k].astype(jnp.float32)
 
     parts = []
-    for k, j in enumerate(order, 1):
+    for at, k in enumerate(sends):
         sent = merged(k).astype(jnp.bfloat16)
-        parts.append(shift(sent, "kv", -2 * j))
-        after = (k + 1) % lines
+        parts.append(shift(sent, "kv", -2 * order[k - 1]))
+        after = (sends + [0])[at + 1]
         arrived[after], _ = lax.optimization_barrier((arrived[after], sent))
     total = merged(0)
     for part in parts:

time: 51.5 us -> 53 us (1.029)
  waiting for transfers between devices: 17.6 us -> 20.4 us
  starting transfers between devices: 19.9 us -> 18.6 us
    ppermute x6, waiting for transfers between devices: 7.29 us -> 9.55 us  [shift(): return lax.ppermute(x, axis, [(i, (i + by) % n) for i in range(n)])]
    ppermute x6, starting transfers between devices: 9.2 us -> 7.96 us  [shift(): return lax.ppermute(x, axis, [(i, (i + by) % n) for i in range(n)])]
    pallas_call x1, Pallas kernels: 3.84 us -> 2.89 us  [attn(): pl.pallas_call(lambda *refs: attn_kernel(sizes, groups, list(scored), hel...]
    pallas_call x2 -> x3, Pallas kernels: 1.71 us -> 2.56 us  [score(): pl.pallas_call(lambda *refs: score_kernel(math.log2(math.e) / math.sqrt(D...]
    ppermute x14, waiting for transfers between devices: 10.3 us -> 10.9 us  [swap(): return lax.ppermute(x, axis, [(i, i ^ bit) for i in range(n)])]
  transfers between devices with their start and end apart: 20 -> 20, of which waited for: 9 -> 12; matrix products, arithmetic and copies ran while one was open for 8% -> 8% of each run, Pallas kernels for 7% -> 8%
where the time goes in v2:
time: 53 us; the launch traced here: 52.7 us
  waiting for transfers between devices  20.4 us (38%)
  starting transfers between devices  18.6 us (35%)
  Pallas kernels  7.16 us (14%)
  local copies, waits for them, and re-layouts  3.84 us (7%)
  other arithmetic  1.8 us (3%)
  between operations  0.85 us (2%)
    ppermute x14, waiting for transfers between devices, swap(): return lax.ppermute(x, axis, [(i, i ^ bit) for i in range(n)])  10.9 us
    ppermute x14, starting transfers between devices, swap(): return lax.ppermute(x, axis, [(i, i ^ bit) for i in range(n)])  10.6 us
    ppermute x6, waiting for transfers between devices, shift(): return lax.ppermute(x, axis, [(i, (i + by) % n) for i in range(n)])  9.55 us
    ppermute x6, starting transfers between devices, shift(): return lax.ppermute(x, axis, [(i, (i + by) % n) for i in range(n)])  7.96 us
    unnamed x10, local copies, waits for them, and re-layouts  3.83 us
    pallas_call x1, Pallas kernels, attn(): pl.pallas_call(lambda *refs: attn_kernel(sizes, groups, list(scored), hel...  2.89 us
    pallas_call x3, Pallas kernels, score(): pl.pallas_call(lambda *refs: score_kernel(math.log2(math.e) / math.sqrt(D...  2.56 us
    pallas_call x2, Pallas kernels, grad(): pl.pallas_call(grad_kernel, in_specs=[vmem] * 8, out_specs=[vmem] * 2, ou...  1.71 us
  transfers between devices with their start and end apart: 20, of which 12 were waited for; matrix products, arithmetic and copies ran while one was open for 8% of the time, Pallas kernels for 8%

profile of v2, /device:TPU:0, one launch (start us, length us, event | category | flops | bytes accessed | tf_op | source)
XLA Modules:
  0.0 52.7 jit_solution(106384778758590955)
XLA Ops:
  0.6 0.8 %fusion.15 = bf16[64,512]{1,0:T(8,128)(2,1)S(1)} fusion(s32[]{:T(128)S(6)} %select_n.23, bf16[128,256]{1,0:T(8,128)(2,1)} %param.5, bf16[128,256]{1,0:T(8,128)(2,1)} %param.6), kind=kLoop, calls=%fused_computation.29 | loop fusion | flops 131072 | bytes 196612 | tf_op jit(solution)/shard_map/concatenate | solution.py:251
  1.4 5.1 %collective-permute-start.2 = (bf16[64,512]{1,0:T(8,128)(2,1)S(1)}, bf16[64,512]{1,0:T(8,128)(2,1)S(1)}, u32[]{:S(2)}, u32[]{:S(2)}) collective-permute-start(bf16[64,512]{1,0:T(8,128)(2,1)S(1)} %fusion.15), channel_id=1, source_target_pairs={{0,6},{1,7},{2,0},{3,1},{4,2},{5,3},{6,4},{7,5},{8,14},{9,15},{10,... | collective-permute-start | bytes 196616 | tf_op jit(solution)/shard_map/ppermute | solution.py:23
  6.5 1.0 %collective-permute-start = (bf16[64,512]{1,0:T(8,128)(2,1)S(1)}, bf16[64,512]{1,0:T(8,128)(2,1)S(1)}, u32[]{:S(2)}, u32[]{:S(2)}) collective-permute-start(bf16[64,512]{1,0:T(8,128)(2,1)S(1)} %fusion.15), channel_id=1, source_target_pairs={{0,4},{1,5},{2,6},{3,7},{4,0},{5,1},{6,2},{7,3},{8,12},{9,13},{10,... | collective-permute-start | bytes 196616 | tf_op jit(solution)/shard_map/ppermute | solution.py:23
  7.5 1.2 %copy.7 = bf16[1024,256]{0,1:T(8,128)(2,1)S(1)} copy(bf16[1024,256]{1,0:T(8,128)(2,1)} %refs_0_.5) | data formatting | bytes 1048576 | tf_op args[0]
  8.8 1.2 %copy.8 = bf16[1024,256]{0,1:T(8,128)(2,1)S(1)} copy(bf16[1024,256]{1,0:T(8,128)(2,1)} %refs_1_.5) | data formatting | bytes 1048576 | tf_op args[3]
  10.0 2.6 %collective-permute-done.1 = bf16[64,512]{1,0:T(8,128)(2,1)S(1)} collective-permute-done((bf16[64,512]{1,0:T(8,128)(2,1)S(1)}, bf16[64,512]{1,0:T(8,128)(2,1)S(1)}, u32[]{:S(2)}, u32[]{:S(2)}) %collective-permute-start.1) | collective-permute-done | bytes 65568 | tf_op jit(solution)/shard_map/ppermute | solution.py:23
  12.7 1.3 %collective-permute-done = bf16[64,512]{1,0:T(8,128)(2,1)S(1)} collective-permute-done((bf16[64,512]{1,0:T(8,128)(2,1)S(1)}, bf16[64,512]{1,0:T(8,128)(2,1)S(1)}, u32[]{:S(2)}, u32[]{:S(2)}) %collective-permute-start) | collective-permute-done | bytes 65568 | tf_op jit(solution)/shard_map/ppermute | solution.py:23
  14.0 0.0 copy-start
  14.0 0.0 copy-start.1
  14.0 0.1 collective-permute-start.7
  14.1 1.6 %collective-permute-start.3 = (bf16[64,512]{1,0:T(8,128)(2,1)S(1)}, bf16[64,512]{1,0:T(8,128)(2,1)S(1)}, u32[]{:S(2)}, u32[]{:S(2)}) collective-permute-start(bf16[64,512]{1,0:T(8,128)(2,1)S(1)} %fusion.15), channel_id=1, source_target_pairs={{0,1},{1,0},{2,3},{3,2},{4,5},{5,4},{6,7},{7,6},{8,9},{9,8},{10,11... | collective-permute-start | bytes 196616 | tf_op jit(solution)/shard_map/ppermute | solution.py:18
  15.7 0.5 collective-permute-start.5
  16.2 1.5 %collective-permute-start.4 = (bf16[64,512]{1,0:T(8,128)(2,1)S(1)}, bf16[64,512]{1,0:T(8,128)(2,1)S(1)}, u32[]{:S(2)}, u32[]{:S(2)}) collective-permute-start(bf16[64,512]{1,0:T(8,128)(2,1)S(1)} %collective-permute-done), channel_id=1, source_target_pairs={{0,1},{1,0},{2,3},{3,2},{4,5},{5,4},{6,7},{7,6},{8,9},{9,8},{10,11... | collective-permute-start | bytes 196616 | tf_op jit(solution)/shard_map/ppermute | solution.py:18
  17.7 0.5 collective-permute-start.6
  18.2 0.9 %shard_map.67 = (f32[512,1024]{1,0:T(8,128)S(1)}, f32[512,1024]{1,0:T(8,128)S(1)}, f32[8,1024]{1,0:T(8,128)S(1)}) custom-call(bf16[256,1024]{1,0:T(8,128)(2,1)S(1)} %bitcast.3, bf16[256,1024]{1,0:T(8,128)(2,1)S(1)} %bitcast.7, bf16[256,512]{1,0:T(8,128)(2,1)S(1)} %pad_maximum_fusion.refs_2_.refs_7_), custom_call_target="tpu_custom_call" | custom-call | flops 268435456 | bytes 2097152 | tf_op jit(solution)/shard_map/pallas_call | solution.py:51
  19.1 0.9 %shard_map.68 = (f32[512,1024]{1,0:T(8,128)S(1)}, f32[512,1024]{1,0:T(8,128)S(1)}, f32[8,1024]{1,0:T(8,128)S(1)}) custom-call(bf16[256,1024]{1,0:T(8,128)(2,1)S(1)} %bitcast.4, bf16[256,1024]{1,0:T(8,128)(2,1)S(1)} %bitcast.8, bf16[256,512]{1,0:T(8,128)(2,1)S(1)} %collective-permute-done.7.refs_2_.refs_5_), custom_call_target="tpu_custom_call" | custom-call | flops 268435456 | bytes 2097152 | tf_op jit(solution)/shard_map/pallas_call | solution.py:51
  19.9 0.7 %collective-permute-done.5 = bf16[64,512]{1,0:T(8,128)(2,1)S(1)} collective-permute-done((bf16[64,512]{1,0:T(8,128)(2,1)S(1)}, bf16[64,512]{1,0:T(8,128)(2,1)S(1)}, u32[]{:S(2)}, u32[]{:S(2)}) %collective-permute-start.5) | collective-permute-done | bytes 65568 | tf_op jit(solution)/shard_map/ppermute | solution.py:18
  20.6 1.4 %collective-permute-done.4 = bf16[64,512]{1,0:T(8,128)(2,1)S(1)} collective-permute-done((bf16[64,512]{1,0:T(8,128)(2,1)S(1)}, bf16[64,512]{1,0:T(8,128)(2,1)S(1)}, u32[]{:S(2)}, u32[]{:S(2)}) %collective-permute-start.4) | collective-permute-done | bytes 65568 | tf_op jit(solution)/shard_map/ppermute | solution.py:18
  22.0 0.8 %collective-permute-done.6 = bf16[64,512]{1,0:T(8,128)(2,1)S(1)} collective-permute-done((bf16[64,512]{1,0:T(8,128)(2,1)S(1)}, bf16[64,512]{1,0:T(8,128)(2,1)S(1)}, u32[]{:S(2)}, u32[]{:S(2)}) %collective-permute-start.6) | collective-permute-done | bytes 65568 | tf_op jit(solution)/shard_map/ppermute | solution.py:18
  22.8 0.1 collective-permute-start.8
  22.9 0.9 %shard_map.69 = (f32[512,1024]{1,0:T(8,128)S(1)}, f32[512,1024]{1,0:T(8,128)S(1)}, f32[8,1024]{1,0:T(8,128)S(1)}) custom-call(bf16[256,1024]{1,0:T(8,128)(2,1)S(1)} %bitcast.5, bf16[256,1024]{1,0:T(8,128)(2,1)S(1)} %bitcast.9, bf16[256,512]{1,0:T(8,128)(2,1)S(1)} %constant_dynamic-update-slice_fusion.refs_2_.refs_6_), custom_call_target="tpu_custom_call" | custom-call | flops 268435456 | bytes 2097152 | tf_op jit(solution)/shard_map/pallas_call | solution.py:51
  23.8 0.7 %collective-permute-done.8.refs_4_ = bf16[256,512]{1,0:T(8,128)(2,1)S(1)} collective-permute-done((bf16[256,512]{1,0:T(8,128)(2,1)S(1)}, bf16[256,512]{1,0:T(8,128)(2,1)S(1)}, u32[]{:S(2)}, u32[]{:S(2)}) %collective-permute-start.8) | collective-permute-done | bytes 262176 | tf_op jit(solution)/shard_map/ppermute | solution.py:18
  24.5 2.9 %shard_map.70 = (f32[256,1024]{1,0:T(8,128)S(1)}, f32[256,512]{1,0:T(8,128)S(1)}, f32[256,512]{1,0:T(8,128)S(1)}, f32[8,1024]{1,0:T(8,128)S(1)}) custom-call(bf16[1024,256]{1,0:T(8,128)(2,1)S(1)} %copy-done, bf16[1024,256]{1,0:T(8,128)(2,1)S(1)} %copy-done.1, bf16[256,1024]{1,0:T(8,128)(2,1)S(1)} %bitcast.6, bf16[256,1024]{1,0:T(8,128)(2,1)S(1)} %bitcast.10, ...), custom_call_target="tpu_custom_call" | custom-call | flops 2684354560 | bytes 2097152 | tf_op jit(solution)/shard_map/pallas_call | solution.py:222
  27.3 0.2 collective-permute-start.10
  27.6 0.4 collective-permute-start.9
  27.9 0.9 %shard_map.71 = (f32[256,1024]{1,0:T(8,128)S(1)}, f32[256,512]{1,0:T(8,128)S(1)}) custom-call(bf16[1024,256]{1,0:T(8,128)(2,1)S(1)} %copy-done, bf16[1024,256]{1,0:T(8,128)(2,1)S(1)} %copy-done.1, bf16[256,512]{1,0:T(8,128)(2,1)S(1)} %constant_dynamic-update-slice_fusion.refs_2_.refs_6_, f32[512,1024]{1,0:T(8,128)S(1)} %get-tuple-element.43.refs_14_.refs_3_, ...), custom_call_target="tpu_custom_call" | custom-call | flops 402653184 | bytes 2097152 | tf_op jit(solution)/shard_map/pallas_call | solution.py:84
  28.8 0.5 %collective-permute-done.10 = f32[256,512]{1,0:T(8,128)S(1)} collective-permute-done((f32[256,512]{1,0:T(8,128)S(1)}, f32[256,512]{1,0:T(8,128)S(1)}, u32[]{:S(2)}, u32[]{:S(2)}) %collective-permute-start.10) | collective-permute-done | bytes 524320 | tf_op jit(solution)/shard_map/ppermute | solution.py:18
  29.3 0.1 fusion.10
  29.4 1.6 %collective-permute-start.14 = (bf16[64,512]{1,0:T(8,128)(2,1)S(1)}, bf16[64,512]{1,0:T(8,128)(2,1)S(1)}, u32[]{:S(2)}, u32[]{:S(2)}) collective-permute-start(bf16[64,512]{1,0:T(8,128)(2,1)S(1)} %get-tuple-element.61), channel_id=1, source_target_pairs={{0,1},{1,0},{2,3},{3,2},{4,5},{5,4},{6,7},{7,6},{8,9},{9,8},{10,11... | collective-permute-start | bytes 196616 | tf_op jit(solution)/shard_map/ppermute | solution.py:18
  31.0 0.9 %shard_map.72 = (f32[256,1024]{1,0:T(8,128)S(1)}, f32[256,512]{1,0:T(8,128)S(1)}) custom-call(bf16[1024,256]{1,0:T(8,128)(2,1)S(1)} %copy-done, bf16[1024,256]{1,0:T(8,128)(2,1)S(1)} %copy-done.1, bf16[256,512]{1,0:T(8,128)(2,1)S(1)} %pad_maximum_fusion.refs_2_.refs_7_, f32[512,1024]{1,0:T(8,128)S(1)} %get-tuple-element.33.refs_8_.refs_3_, ...), custom_call_target="tpu_custom_call" | custom-call | flops 402653184 | bytes 2097152 | tf_op jit(solution)/shard_map/pallas_call | solution.py:84
  31.9 0.6 %collective-permute-start.11 = (bf16[64,512]{1,0:T(8,128)(2,1)S(1)}, bf16[64,512]{1,0:T(8,128)(2,1)S(1)}, u32[]{:S(2)}, u32[]{:S(2)}) collective-permute-start(bf16[64,512]{1,0:T(8,128)(2,1)S(1)} %get-tuple-element.60), channel_id=1, source_target_pairs={{0,1},{1,0},{2,3},{3,2},{4,5},{5,4},{6,7},{7,6},{8,9},{9,8},{10,11... | collective-permute-start | bytes 196616 | tf_op jit(solution)/shard_map/ppermute | solution.py:18
  32.4 1.5 %collective-permute-start.13 = (bf16[64,512]{1,0:T(8,128)(2,1)S(1)}, bf16[64,512]{1,0:T(8,128)(2,1)S(1)}, u32[]{:S(2)}, u32[]{:S(2)}) collective-permute-start(bf16[64,512]{1,0:T(8,128)(2,1)S(1)} %get-tuple-element.62), channel_id=1, source_target_pairs={{0,1},{1,0},{2,3},{3,2},{4,5},{5,4},{6,7},{7,6},{8,9},{9,8},{10,11... | collective-permute-start | bytes 196616 | tf_op jit(solution)/shard_map/ppermute | solution.py:18
  34.0 0.5 collective-permute-start.12
  34.5 0.0 collective-permute-done.9
  34.5 0.1 collective-permute-start.15
  34.6 3.3 %collective-permute-done.13 = bf16[64,512]{1,0:T(8,128)(2,1)S(1)} collective-permute-done((bf16[64,512]{1,0:T(8,128)(2,1)S(1)}, bf16[64,512]{1,0:T(8,128)(2,1)S(1)}, u32[]{:S(2)}, u32[]{:S(2)}) %collective-permute-start.13) | collective-permute-done | bytes 65568 | tf_op jit(solution)/shard_map/ppermute | solution.py:18
  37.9 1.7 %collective-permute-start.16 = (bf16[64,512]{1,0:T(8,128)(2,1)S(1)}, bf16[64,512]{1,0:T(8,128)(2,1)S(1)}, u32[]{:S(2)}, u32[]{:S(2)}) collective-permute-start(bf16[64,512]{1,0:T(8,128)(2,1)S(1)} %fusion.6), channel_id=1, source_target_pairs={{0,6},{1,7},{2,0},{3,1},{4,2},{5,3},{6,4},{7,5},{8,14},{9,15},{10,... | collective-permute-start | bytes 196616 | tf_op jit(solution)/shard_map/ppermute | solution.py:23
  39.7 0.1 collective-permute-start.17
  39.8 0.8 %collective-permute-done.15 = bf16[64,512]{1,0:T(8,128)(2,1)S(1)} collective-permute-done((bf16[64,512]{1,0:T(8,128)(2,1)S(1)}, bf16[64,512]{1,0:T(8,128)(2,1)S(1)}, u32[]{:S(2)}, u32[]{:S(2)}) %collective-permute-start.15) | collective-permute-done | bytes 65568 | tf_op jit(solution)/shard_map/ppermute | solution.py:23
  40.6 1.9 %collective-permute-done.16 = bf16[64,512]{1,0:T(8,128)(2,1)S(1)} collective-permute-done((bf16[64,512]{1,0:T(8,128)(2,1)S(1)}, bf16[64,512]{1,0:T(8,128)(2,1)S(1)}, u32[]{:S(2)}, u32[]{:S(2)}) %collective-permute-start.16) | collective-permute-done | bytes 65568 | tf_op jit(solution)/shard_map/ppermute | solution.py:23
  42.6 2.8 %collective-permute-done.17 = bf16[64,512]{1,0:T(8,128)(2,1)S(1)} collective-permute-done((bf16[64,512]{1,0:T(8,128)(2,1)S(1)}, bf16[64,512]{1,0:T(8,128)(2,1)S(1)}, u32[]{:S(2)}, u32[]{:S(2)}) %collective-permute-start.17) | collective-permute-done | bytes 65568 | tf_op jit(solution)/shard_map/ppermute | solution.py:23
  45.4 0.1 fusion.14
  45.5 1.6 %collective-permute-start.18 = (f32[64,512]{1,0:T(8,128)S(1)}, f32[64,512]{1,0:T(8,128)S(1)}, u32[]{:S(2)}, u32[]{:S(2)}) collective-permute-start(f32[64,512]{1,0:T(8,128)S(1)} %fusion.14), channel_id=1, source_target_pairs={{0,16},{8,24},{16,0},{24,8},{1,17},{9,25},{17,1},{25,9},{2,18},{10... | collective-permute-start | bytes 393224 | tf_op jit(solution)/shard_map/ppermute | solution.py:18
  47.0 3.5 %collective-permute-done.18 = f32[64,512]{1,0:T(8,128)S(1)} collective-permute-done((f32[64,512]{1,0:T(8,128)S(1)}, f32[64,512]{1,0:T(8,128)S(1)}, u32[]{:S(2)}, u32[]{:S(2)}) %collective-permute-start.18) | collective-permute-done | bytes 131104 | tf_op jit(solution)/shard_map/ppermute | solution.py:18
  50.5 0.1 collective-permute-start.19
  50.6 1.3 %copy.9 = f32[1024,256]{1,0:T(8,128)} copy(f32[1024,256]{0,1:T(8,128)S(1)} %bitcast.11) | data formatting | bytes 2097152
  51.9 0.0 collective-permute-done.19
  52.0 0.7 %pad_maximum_fusion.1 = (f32[128,256]{1,0:T(8,128)}, f32[128,256]{1,0:T(8,128)}) fusion(f32[64,512]{1,0:T(8,128)S(1)} %get-tuple-element.66, f32[64,512]{1,0:T(8,128)S(1)} %get-tuple-element.67), kind=kLoop, calls=%fused_computation.4 | loop fusion | flops 65536 | bytes 524288 | tf_op jit(solution)/shard_map/concatenate | solution.py:318
  (19 shorter events, 0.2 us)
Async XLA Ops:
  1.4 8.6 %collective-permute-start.2 = (bf16[64,512]{1,0:T(8,128)(2,1)S(1)}, bf16[64,512]{1,0:T(8,128)(2,1)S(1)}, u32[]{:S(2)}, u32[]{:S(2)}) collective-permute-start(bf16[64,512]{1,0:T(8,128)(2,1)S(1)} %fusion.15), channel_id=1, source_target_pairs={{0,6},{1,7},{2,0},{3,1},{4,2},{5,3},{6,4},{7,5},{8,14},{9,15},{10,... | collective-permute-start | bytes 196616 | tf_op jit(solution)/shard_map/ppermute | solution.py:23
  6.5 6.2 %collective-permute-start.1 = (bf16[64,512]{1,0:T(8,128)(2,1)S(1)}, bf16[64,512]{1,0:T(8,128)(2,1)S(1)}, u32[]{:S(2)}, u32[]{:S(2)}) collective-permute-start(bf16[64,512]{1,0:T(8,128)(2,1)S(1)} %fusion.15), channel_id=1, source_target_pairs={{0,2},{1,3},{2,4},{3,5},{4,6},{5,7},{6,0},{7,1},{8,10},{9,11},{10,... | collective-permute-start | bytes 196616 | tf_op jit(solution)/shard_map/ppermute | solution.py:23
  6.5 7.5 %collective-permute-start = (bf16[64,512]{1,0:T(8,128)(2,1)S(1)}, bf16[64,512]{1,0:T(8,128)(2,1)S(1)}, u32[]{:S(2)}, u32[]{:S(2)}) collective-permute-start(bf16[64,512]{1,0:T(8,128)(2,1)S(1)} %fusion.15), channel_id=1, source_target_pairs={{0,4},{1,5},{2,6},{3,7},{4,0},{5,1},{6,2},{7,3},{8,12},{9,13},{10,... | collective-permute-start | bytes 196616 | tf_op jit(solution)/shard_map/ppermute | solution.py:23
  14.0 10.5 %copy-start = (bf16[1024,256]{1,0:T(8,128)(2,1)S(1)}, bf16[1024,256]{1,0:T(8,128)(2,1)}, u32[]{:S(2)}) copy-start(bf16[1024,256]{1,0:T(8,128)(2,1)} %refs_0_.5) | copy-start | bytes 1572868
  14.0 10.4 %copy-start.1 = (bf16[1024,256]{1,0:T(8,128)(2,1)S(1)}, bf16[1024,256]{1,0:T(8,128)(2,1)}, u32[]{:S(2)}) copy-start(bf16[1024,256]{1,0:T(8,128)(2,1)} %refs_1_.5) | copy-start | bytes 1572868
  14.0 5.1 %collective-permute-start.7 = (bf16[256,512]{1,0:T(8,128)(2,1)S(1)}, bf16[256,512]{1,0:T(8,128)(2,1)S(1)}, u32[]{:S(2)}, u32[]{:S(2)}) collective-permute-start(bf16[256,512]{1,0:T(8,128)(2,1)S(1)} %pad_maximum_fusion.refs_2_.refs_7_), channel_id=1, source_target_pairs={{0,8},{8,0},{16,24},{24,16},{1,9},{9,1},{17,25},{25,17},{2,10},{10... | collective-permute-start | bytes 786440 | tf_op jit(solution)/shard_map/ppermute | solution.py:18
  14.1 5.8 %collective-permute-start.3 = (bf16[64,512]{1,0:T(8,128)(2,1)S(1)}, bf16[64,512]{1,0:T(8,128)(2,1)S(1)}, u32[]{:S(2)}, u32[]{:S(2)}) collective-permute-start(bf16[64,512]{1,0:T(8,128)(2,1)S(1)} %fusion.15), channel_id=1, source_target_pairs={{0,1},{1,0},{2,3},{3,2},{4,5},{5,4},{6,7},{7,6},{8,9},{9,8},{10,11... | collective-permute-start | bytes 196616 | tf_op jit(solution)/shard_map/ppermute | solution.py:18
  15.7 5.0 %collective-permute-start.5 = (bf16[64,512]{1,0:T(8,128)(2,1)S(1)}, bf16[64,512]{1,0:T(8,128)(2,1)S(1)}, u32[]{:S(2)}, u32[]{:S(2)}) collective-permute-start(bf16[64,512]{1,0:T(8,128)(2,1)S(1)} %collective-permute-done.1), channel_id=1, source_target_pairs={{0,1},{1,0},{2,3},{3,2},{4,5},{5,4},{6,7},{7,6},{8,9},{9,8},{10,11... | collective-permute-start | bytes 196616 | tf_op jit(solution)/shard_map/ppermute | solution.py:18
  16.2 5.9 %collective-permute-start.4 = (bf16[64,512]{1,0:T(8,128)(2,1)S(1)}, bf16[64,512]{1,0:T(8,128)(2,1)S(1)}, u32[]{:S(2)}, u32[]{:S(2)}) collective-permute-start(bf16[64,512]{1,0:T(8,128)(2,1)S(1)} %collective-permute-done), channel_id=1, source_target_pairs={{0,1},{1,0},{2,3},{3,2},{4,5},{5,4},{6,7},{7,6},{8,9},{9,8},{10,11... | collective-permute-start | bytes 196616 | tf_op jit(solution)/shard_map/ppermute | solution.py:18
  17.7 5.1 %collective-permute-start.6 = (bf16[64,512]{1,0:T(8,128)(2,1)S(1)}, bf16[64,512]{1,0:T(8,128)(2,1)S(1)}, u32[]{:S(2)}, u32[]{:S(2)}) collective-permute-start(bf16[64,512]{1,0:T(8,128)(2,1)S(1)} %collective-permute-done.2), channel_id=1, source_target_pairs={{0,1},{1,0},{2,3},{3,2},{4,5},{5,4},{6,7},{7,6},{8,9},{9,8},{10,11... | collective-permute-start | bytes 196616 | tf_op jit(solution)/shard_map/ppermute | solution.py:18
  22.8 1.6 %collective-permute-start.8 = (bf16[256,512]{1,0:T(8,128)(2,1)S(1)}, bf16[256,512]{1,0:T(8,128)(2,1)S(1)}, u32[]{:S(2)}, u32[]{:S(2)}) collective-permute-start(bf16[256,512]{1,0:T(8,128)(2,1)S(1)} %constant_dynamic-update-slice_fusion.refs_2_.refs_6_), channel_id=1, source_target_pairs={{0,8},{8,0},{16,24},{24,16},{1,9},{9,1},{17,25},{25,17},{2,10},{10... | collective-permute-start | bytes 786440 | tf_op jit(solution)/shard_map/ppermute | solution.py:18
  27.3 2.0 %collective-permute-start.10 = (f32[256,512]{1,0:T(8,128)S(1)}, f32[256,512]{1,0:T(8,128)S(1)}, u32[]{:S(2)}, u32[]{:S(2)}) collective-permute-start(f32[256,512]{1,0:T(8,128)S(1)} %get-tuple-element.53), channel_id=1, source_target_pairs={{0,8},{8,0},{16,24},{24,16},{1,9},{9,1},{17,25},{25,17},{2,10},{10... | collective-permute-start | bytes 1572872 | tf_op jit(solution)/shard_map/ppermute | solution.py:18
  27.6 6.9 %collective-permute-start.9 = (f32[256,512]{1,0:T(8,128)S(1)}, f32[256,512]{1,0:T(8,128)S(1)}, u32[]{:S(2)}, u32[]{:S(2)}) collective-permute-start(f32[256,512]{1,0:T(8,128)S(1)} %get-tuple-element.51), channel_id=1, source_target_pairs={{0,8},{8,0},{16,24},{24,16},{1,9},{9,1},{17,25},{25,17},{2,10},{10... | collective-permute-start | bytes 1572872 | tf_op jit(solution)/shard_map/ppermute | solution.py:18
  29.4 5.1 %collective-permute-start.14 = (bf16[64,512]{1,0:T(8,128)(2,1)S(1)}, bf16[64,512]{1,0:T(8,128)(2,1)S(1)}, u32[]{:S(2)}, u32[]{:S(2)}) collective-permute-start(bf16[64,512]{1,0:T(8,128)(2,1)S(1)} %get-tuple-element.61), channel_id=1, source_target_pairs={{0,1},{1,0},{2,3},{3,2},{4,5},{5,4},{6,7},{7,6},{8,9},{9,8},{10,11... | collective-permute-start | bytes 196616 | tf_op jit(solution)/shard_map/ppermute | solution.py:18
  31.9 7.9 %collective-permute-start.11 = (bf16[64,512]{1,0:T(8,128)(2,1)S(1)}, bf16[64,512]{1,0:T(8,128)(2,1)S(1)}, u32[]{:S(2)}, u32[]{:S(2)}) collective-permute-start(bf16[64,512]{1,0:T(8,128)(2,1)S(1)} %get-tuple-element.60), channel_id=1, source_target_pairs={{0,1},{1,0},{2,3},{3,2},{4,5},{5,4},{6,7},{7,6},{8,9},{9,8},{10,11... | collective-permute-start | bytes 196616 | tf_op jit(solution)/shard_map/ppermute | solution.py:18
  32.4 5.5 %collective-permute-start.13 = (bf16[64,512]{1,0:T(8,128)(2,1)S(1)}, bf16[64,512]{1,0:T(8,128)(2,1)S(1)}, u32[]{:S(2)}, u32[]{:S(2)}) collective-permute-start(bf16[64,512]{1,0:T(8,128)(2,1)S(1)} %get-tuple-element.62), channel_id=1, source_target_pairs={{0,1},{1,0},{2,3},{3,2},{4,5},{5,4},{6,7},{7,6},{8,9},{9,8},{10,11... | collective-permute-start | bytes 196616 | tf_op jit(solution)/shard_map/ppermute | solution.py:18
  34.0 5.7 %collective-permute-start.12 = (bf16[64,512]{1,0:T(8,128)(2,1)S(1)}, bf16[64,512]{1,0:T(8,128)(2,1)S(1)}, u32[]{:S(2)}, u32[]{:S(2)}) collective-permute-start(bf16[64,512]{1,0:T(8,128)(2,1)S(1)} %get-tuple-element.63), channel_id=1, source_target_pairs={{0,1},{1,0},{2,3},{3,2},{4,5},{5,4},{6,7},{7,6},{8,9},{9,8},{10,11... | collective-permute-start | bytes 196616 | tf_op jit(solution)/shard_map/ppermute | solution.py:18
  34.5 6.1 %collective-permute-start.15 = (bf16[64,512]{1,0:T(8,128)(2,1)S(1)}, bf16[64,512]{1,0:T(8,128)(2,1)S(1)}, u32[]{:S(2)}, u32[]{:S(2)}) collective-permute-start(bf16[64,512]{1,0:T(8,128)(2,1)S(1)} %fusion.3), channel_id=1, source_target_pairs={{0,2},{1,3},{2,4},{3,5},{4,6},{5,7},{6,0},{7,1},{8,10},{9,11},{10,... | collective-permute-start | bytes 196616 | tf_op jit(solution)/shard_map/ppermute | solution.py:23
  37.9 4.6 %collective-permute-start.16 = (bf16[64,512]{1,0:T(8,128)(2,1)S(1)}, bf16[64,512]{1,0:T(8,128)(2,1)S(1)}, u32[]{:S(2)}, u32[]{:S(2)}) collective-permute-start(bf16[64,512]{1,0:T(8,128)(2,1)S(1)} %fusion.6), channel_id=1, source_target_pairs={{0,6},{1,7},{2,0},{3,1},{4,2},{5,3},{6,4},{7,5},{8,14},{9,15},{10,... | collective-permute-start | bytes 196616 | tf_op jit(solution)/shard_map/ppermute | solution.py:23
  39.7 5.7 %collective-permute-start.17 = (bf16[64,512]{1,0:T(8,128)(2,1)S(1)}, bf16[64,512]{1,0:T(8,128)(2,1)S(1)}, u32[]{:S(2)}, u32[]{:S(2)}) collective-permute-start(bf16[64,512]{1,0:T(8,128)(2,1)S(1)} %fusion.9), channel_id=1, source_target_pairs={{0,4},{1,5},{2,6},{3,7},{4,0},{5,1},{6,2},{7,3},{8,12},{9,13},{10,... | collective-permute-start | bytes 196616 | tf_op jit(solution)/shard_map/ppermute | solution.py:23
  45.5 5.0 %collective-permute-start.18 = (f32[64,512]{1,0:T(8,128)S(1)}, f32[64,512]{1,0:T(8,128)S(1)}, u32[]{:S(2)}, u32[]{:S(2)}) collective-permute-start(f32[64,512]{1,0:T(8,128)S(1)} %fusion.14), channel_id=1, source_target_pairs={{0,16},{8,24},{16,0},{24,8},{1,17},{9,25},{17,1},{25,9},{2,18},{10... | collective-permute-start | bytes 393224 | tf_op jit(solution)/shard_map/ppermute | solution.py:18
  50.5 1.4 %collective-permute-start.19 = (f32[64,512]{1,0:T(8,128)S(1)}, f32[64,512]{1,0:T(8,128)S(1)}, u32[]{:S(2)}, u32[]{:S(2)}) collective-permute-start(f32[64,512]{1,0:T(8,128)S(1)} %add.72), channel_id=1, source_target_pairs={{0,8},{8,0},{16,24},{24,16},{1,9},{9,1},{17,25},{25,17},{2,10},{10... | collective-permute-start | bytes 393224 | tf_op jit(solution)/shard_map/ppermute | solution.py:18

commit v3 on v2

--- a/solution.py
+++ b/solution.py
@@ -272,10 +272,11 @@
         scored[2] = score(queries_t, dout_t, far_all)
     pieces, groups = [far_o, near_o, far_all, near], [many] * 4
     if early:
-        dq, g_far_o, g_near_o, stat = attn(
-            queries, dout, queries_t, dout_t, pieces, groups, scored, [2, 3]
+        dq, g_far_o, stat = attn(
+            queries, dout, queries_t, dout_t, [far_o], [many], scored, [1, 2, 3]
         )
         g_far_o = swap(g_far_o, "pb", 1)
+        dq, g_near_o = grad(queries, dout, near_o, *scored[1], stat, dq)
         g_near_o = swap(g_near_o, "pb", 1)
         dq, g_far = grad(queries, dout, far_all, *scored[2], stat, dq)
         dq, g_near = grad(queries, dout, near, *scored[3], stat, dq)

time: 53 us -> 52.7 us (level)
    pallas_call x2 -> x3, Pallas kernels: 1.71 us -> 2.57 us  [grad(): pl.pallas_call(grad_kernel, in_specs=[vmem] * 8, out_specs=[vmem] * 2, ou...]
    pallas_call x1, Pallas kernels: 2.89 us -> 2.21 us  [attn(): pl.pallas_call(lambda *refs: attn_kernel(sizes, groups, list(scored), hel...]
    ppermute x14, waiting for transfers between devices: 10.9 us -> 10.3 us  [swap(): return lax.ppermute(x, axis, [(i, i ^ bit) for i in range(n)])]
  transfers between devices with their start and end apart: 20 -> 20, of which waited for: 12 -> 11; matrix products, arithmetic and copies ran while one was open for 8% -> 8% of each run, Pallas kernels for 8% -> 10%
where the time goes in v3:
time: 52.7 us; the launch traced here: 52.4 us
  waiting for transfers between devices  19.9 us (38%)
  starting transfers between devices  18.7 us (35%)
  Pallas kernels  7.33 us (14%)
  local copies, waits for them, and re-layouts  3.84 us (7%)
  other arithmetic  1.77 us (3%)
  between operations  0.87 us (2%)
    ppermute x14, starting transfers between devices, swap(): return lax.ppermute(x, axis, [(i, i ^ bit) for i in range(n)])  10.7 us
    ppermute x14, waiting for transfers between devices, swap(): return lax.ppermute(x, axis, [(i, i ^ bit) for i in range(n)])  10.3 us
    ppermute x6, waiting for transfers between devices, shift(): return lax.ppermute(x, axis, [(i, (i + by) % n) for i in range(n)])  9.54 us
    ppermute x6, starting transfers between devices, shift(): return lax.ppermute(x, axis, [(i, (i + by) % n) for i in range(n)])  7.96 us
    unnamed x10, local copies, waits for them, and re-layouts  3.83 us
    pallas_call x3, Pallas kernels, grad(): pl.pallas_call(grad_kernel, in_specs=[vmem] * 8, out_specs=[vmem] * 2, ou...  2.57 us
    pallas_call x3, Pallas kernels, score(): pl.pallas_call(lambda *refs: score_kernel(math.log2(math.e) / math.sqrt(D...  2.56 us
    pallas_call x1, Pallas kernels, attn(): pl.pallas_call(lambda *refs: attn_kernel(sizes, groups, list(scored), hel...  2.21 us
  transfers between devices with their start and end apart: 20, of which 11 were waited for; matrix products, arithmetic and copies ran while one was open for 8% of the time, Pallas kernels for 10%

profile of v3, /device:TPU:0, one launch (start us, length us, event | category | flops | bytes accessed | tf_op | source)
XLA Modules:
  0.0 52.4 jit_solution(14143447391578499417)
XLA Ops:
  0.6 0.8 %fusion.15 = bf16[64,512]{1,0:T(8,128)(2,1)S(1)} fusion(s32[]{:T(128)S(6)} %select_n.23, bf16[128,256]{1,0:T(8,128)(2,1)} %param.5, bf16[128,256]{1,0:T(8,128)(2,1)} %param.6), kind=kLoop, calls=%fused_computation.29 | loop fusion | flops 131072 | bytes 196612 | tf_op jit(solution)/shard_map/concatenate | solution.py:251
  1.4 5.1 %collective-permute-start.2 = (bf16[64,512]{1,0:T(8,128)(2,1)S(1)}, bf16[64,512]{1,0:T(8,128)(2,1)S(1)}, u32[]{:S(2)}, u32[]{:S(2)}) collective-permute-start(bf16[64,512]{1,0:T(8,128)(2,1)S(1)} %fusion.15), channel_id=1, source_target_pairs={{0,6},{1,7},{2,0},{3,1},{4,2},{5,3},{6,4},{7,5},{8,14},{9,15},{10,... | collective-permute-start | bytes 196616 | tf_op jit(solution)/shard_map/ppermute | solution.py:23
  6.5 1.0 %collective-permute-start = (bf16[64,512]{1,0:T(8,128)(2,1)S(1)}, bf16[64,512]{1,0:T(8,128)(2,1)S(1)}, u32[]{:S(2)}, u32[]{:S(2)}) collective-permute-start(bf16[64,512]{1,0:T(8,128)(2,1)S(1)} %fusion.15), channel_id=1, source_target_pairs={{0,4},{1,5},{2,6},{3,7},{4,0},{5,1},{6,2},{7,3},{8,12},{9,13},{10,... | collective-permute-start | bytes 196616 | tf_op jit(solution)/shard_map/ppermute | solution.py:23
  7.5 1.2 %copy.7 = bf16[1024,256]{0,1:T(8,128)(2,1)S(1)} copy(bf16[1024,256]{1,0:T(8,128)(2,1)} %refs_0_.7) | data formatting | bytes 1048576 | tf_op args[0]
  8.8 1.2 %copy.8 = bf16[1024,256]{0,1:T(8,128)(2,1)S(1)} copy(bf16[1024,256]{1,0:T(8,128)(2,1)} %refs_1_.7) | data formatting | bytes 1048576 | tf_op args[3]
  10.0 2.6 %collective-permute-done.1 = bf16[64,512]{1,0:T(8,128)(2,1)S(1)} collective-permute-done((bf16[64,512]{1,0:T(8,128)(2,1)S(1)}, bf16[64,512]{1,0:T(8,128)(2,1)S(1)}, u32[]{:S(2)}, u32[]{:S(2)}) %collective-permute-start.1) | collective-permute-done | bytes 65568 | tf_op jit(solution)/shard_map/ppermute | solution.py:23
  12.7 1.3 %collective-permute-done = bf16[64,512]{1,0:T(8,128)(2,1)S(1)} collective-permute-done((bf16[64,512]{1,0:T(8,128)(2,1)S(1)}, bf16[64,512]{1,0:T(8,128)(2,1)S(1)}, u32[]{:S(2)}, u32[]{:S(2)}) %collective-permute-start) | collective-permute-done | bytes 65568 | tf_op jit(solution)/shard_map/ppermute | solution.py:23
  14.0 0.0 copy-start
  14.0 0.0 copy-start.1
  14.0 0.1 collective-permute-start.7
  14.1 1.6 %collective-permute-start.3 = (bf16[64,512]{1,0:T(8,128)(2,1)S(1)}, bf16[64,512]{1,0:T(8,128)(2,1)S(1)}, u32[]{:S(2)}, u32[]{:S(2)}) collective-permute-start(bf16[64,512]{1,0:T(8,128)(2,1)S(1)} %fusion.15), channel_id=1, source_target_pairs={{0,1},{1,0},{2,3},{3,2},{4,5},{5,4},{6,7},{7,6},{8,9},{9,8},{10,11... | collective-permute-start | bytes 196616 | tf_op jit(solution)/shard_map/ppermute | solution.py:18
  15.7 0.5 collective-permute-start.5
  16.2 1.5 %collective-permute-start.4 = (bf16[64,512]{1,0:T(8,128)(2,1)S(1)}, bf16[64,512]{1,0:T(8,128)(2,1)S(1)}, u32[]{:S(2)}, u32[]{:S(2)}) collective-permute-start(bf16[64,512]{1,0:T(8,128)(2,1)S(1)} %collective-permute-done), channel_id=1, source_target_pairs={{0,1},{1,0},{2,3},{3,2},{4,5},{5,4},{6,7},{7,6},{8,9},{9,8},{10,11... | collective-permute-start | bytes 196616 | tf_op jit(solution)/shard_map/ppermute | solution.py:18
  17.7 0.5 collective-permute-start.6
  18.2 0.9 %shard_map.67 = (f32[512,1024]{1,0:T(8,128)S(1)}, f32[512,1024]{1,0:T(8,128)S(1)}, f32[8,1024]{1,0:T(8,128)S(1)}) custom-call(bf16[256,1024]{1,0:T(8,128)(2,1)S(1)} %bitcast.3, bf16[256,1024]{1,0:T(8,128)(2,1)S(1)} %bitcast.7, bf16[256,512]{1,0:T(8,128)(2,1)S(1)} %pad_maximum_fusion.refs_2_), custom_call_target="tpu_custom_call" | custom-call | flops 268435456 | bytes 2097152 | tf_op jit(solution)/shard_map/pallas_call | solution.py:51
  19.1 0.9 %shard_map.68 = (f32[512,1024]{1,0:T(8,128)S(1)}, f32[512,1024]{1,0:T(8,128)S(1)}, f32[8,1024]{1,0:T(8,128)S(1)}) custom-call(bf16[256,1024]{1,0:T(8,128)(2,1)S(1)} %bitcast.4, bf16[256,1024]{1,0:T(8,128)(2,1)S(1)} %bitcast.8, bf16[256,512]{1,0:T(8,128)(2,1)S(1)} %collective-permute-done.7.refs_2_), custom_call_target="tpu_custom_call" | custom-call | flops 268435456 | bytes 2097152 | tf_op jit(solution)/shard_map/pallas_call | solution.py:51
  19.9 0.7 %collective-permute-done.5 = bf16[64,512]{1,0:T(8,128)(2,1)S(1)} collective-permute-done((bf16[64,512]{1,0:T(8,128)(2,1)S(1)}, bf16[64,512]{1,0:T(8,128)(2,1)S(1)}, u32[]{:S(2)}, u32[]{:S(2)}) %collective-permute-start.5) | collective-permute-done | bytes 65568 | tf_op jit(solution)/shard_map/ppermute | solution.py:18
  20.6 1.4 %collective-permute-done.4 = bf16[64,512]{1,0:T(8,128)(2,1)S(1)} collective-permute-done((bf16[64,512]{1,0:T(8,128)(2,1)S(1)}, bf16[64,512]{1,0:T(8,128)(2,1)S(1)}, u32[]{:S(2)}, u32[]{:S(2)}) %collective-permute-start.4) | collective-permute-done | bytes 65568 | tf_op jit(solution)/shard_map/ppermute | solution.py:18
  22.0 0.8 %collective-permute-done.6 = bf16[64,512]{1,0:T(8,128)(2,1)S(1)} collective-permute-done((bf16[64,512]{1,0:T(8,128)(2,1)S(1)}, bf16[64,512]{1,0:T(8,128)(2,1)S(1)}, u32[]{:S(2)}, u32[]{:S(2)}) %collective-permute-start.6) | collective-permute-done | bytes 65568 | tf_op jit(solution)/shard_map/ppermute | solution.py:18
  22.8 0.1 collective-permute-start.8
  22.9 0.9 %shard_map.69 = (f32[512,1024]{1,0:T(8,128)S(1)}, f32[512,1024]{1,0:T(8,128)S(1)}, f32[8,1024]{1,0:T(8,128)S(1)}) custom-call(bf16[256,1024]{1,0:T(8,128)(2,1)S(1)} %bitcast.5, bf16[256,1024]{1,0:T(8,128)(2,1)S(1)} %bitcast.9, bf16[256,512]{1,0:T(8,128)(2,1)S(1)} %constant_dynamic-update-slice_fusion.refs_2_), custom_call_target="tpu_custom_call" | custom-call | flops 268435456 | bytes 2097152 | tf_op jit(solution)/shard_map/pallas_call | solution.py:51
  23.8 0.7 %collective-permute-done.8.refs_4_ = bf16[256,512]{1,0:T(8,128)(2,1)S(1)} collective-permute-done((bf16[256,512]{1,0:T(8,128)(2,1)S(1)}, bf16[256,512]{1,0:T(8,128)(2,1)S(1)}, u32[]{:S(2)}, u32[]{:S(2)}) %collective-permute-start.8) | collective-permute-done | bytes 262176 | tf_op jit(solution)/shard_map/ppermute | solution.py:18
  24.5 2.2 %shard_map.70 = (f32[256,1024]{1,0:T(8,128)S(1)}, f32[256,512]{1,0:T(8,128)S(1)}, f32[8,1024]{1,0:T(8,128)S(1)}) custom-call(bf16[1024,256]{1,0:T(8,128)(2,1)S(1)} %copy-done, bf16[1024,256]{1,0:T(8,128)(2,1)S(1)} %copy-done.1, bf16[256,1024]{1,0:T(8,128)(2,1)S(1)} %bitcast.6, bf16[256,1024]{1,0:T(8,128)(2,1)S(1)} %bitcast.10, ...), custom_call_target="tpu_custom_call" | custom-call | flops 671088640 | bytes 2097152 | tf_op jit(solution)/shard_map/pallas_call | solution.py:222
  26.7 0.2 collective-permute-start.10
  26.9 0.9 %shard_map.71 = (f32[256,1024]{1,0:T(8,128)S(1)}, f32[256,512]{1,0:T(8,128)S(1)}) custom-call(bf16[1024,256]{1,0:T(8,128)(2,1)S(1)} %copy-done, bf16[1024,256]{1,0:T(8,128)(2,1)S(1)} %copy-done.1, bf16[256,512]{1,0:T(8,128)(2,1)S(1)} %collective-permute-done.7.refs_2_, f32[512,1024]{1,0:T(8,128)S(1)} %get-tuple-element.42.refs_8_.refs_3_, ...), custom_call_target="tpu_custom_call" | custom-call | flops 402653184 | bytes 2097152 | tf_op jit(solution)/shard_map/pallas_call | solution.py:84
  27.7 0.4 collective-permute-start.9
  28.2 0.9 %shard_map.72 = (f32[256,1024]{1,0:T(8,128)S(1)}, f32[256,512]{1,0:T(8,128)S(1)}) custom-call(bf16[1024,256]{1,0:T(8,128)(2,1)S(1)} %copy-done, bf16[1024,256]{1,0:T(8,128)(2,1)S(1)} %copy-done.1, bf16[256,512]{1,0:T(8,128)(2,1)S(1)} %constant_dynamic-update-slice_fusion.refs_2_, f32[512,1024]{1,0:T(8,128)S(1)} %get-tuple-element.44.refs_11_.refs_3_, ...), custom_call_target="tpu_custom_call" | custom-call | flops 402653184 | bytes 2097152 | tf_op jit(solution)/shard_map/pallas_call | solution.py:84
  29.0 0.0 collective-permute-done.10
  29.0 0.1 fusion.10
  29.1 1.6 %collective-permute-start.14 = (bf16[64,512]{1,0:T(8,128)(2,1)S(1)}, bf16[64,512]{1,0:T(8,128)(2,1)S(1)}, u32[]{:S(2)}, u32[]{:S(2)}) collective-permute-start(bf16[64,512]{1,0:T(8,128)(2,1)S(1)} %get-tuple-element.63), channel_id=1, source_target_pairs={{0,1},{1,0},{2,3},{3,2},{4,5},{5,4},{6,7},{7,6},{8,9},{9,8},{10,11... | collective-permute-start | bytes 196616 | tf_op jit(solution)/shard_map/ppermute | solution.py:18
  30.7 0.9 %shard_map.73 = (f32[256,1024]{1,0:T(8,128)S(1)}, f32[256,512]{1,0:T(8,128)S(1)}) custom-call(bf16[1024,256]{1,0:T(8,128)(2,1)S(1)} %copy-done, bf16[1024,256]{1,0:T(8,128)(2,1)S(1)} %copy-done.1, bf16[256,512]{1,0:T(8,128)(2,1)S(1)} %pad_maximum_fusion.refs_2_, f32[512,1024]{1,0:T(8,128)S(1)} %get-tuple-element.34.refs_5_.refs_3_, ...), custom_call_target="tpu_custom_call" | custom-call | flops 402653184 | bytes 2097152 | tf_op jit(solution)/shard_map/pallas_call | solution.py:84
  31.6 0.6 %collective-permute-start.11 = (bf16[64,512]{1,0:T(8,128)(2,1)S(1)}, bf16[64,512]{1,0:T(8,128)(2,1)S(1)}, u32[]{:S(2)}, u32[]{:S(2)}) collective-permute-start(bf16[64,512]{1,0:T(8,128)(2,1)S(1)} %get-tuple-element.62), channel_id=1, source_target_pairs={{0,1},{1,0},{2,3},{3,2},{4,5},{5,4},{6,7},{7,6},{8,9},{9,8},{10,11... | collective-permute-start | bytes 196616 | tf_op jit(solution)/shard_map/ppermute | solution.py:18
  32.2 1.5 %collective-permute-start.13 = (bf16[64,512]{1,0:T(8,128)(2,1)S(1)}, bf16[64,512]{1,0:T(8,128)(2,1)S(1)}, u32[]{:S(2)}, u32[]{:S(2)}) collective-permute-start(bf16[64,512]{1,0:T(8,128)(2,1)S(1)} %get-tuple-element.64), channel_id=1, source_target_pairs={{0,1},{1,0},{2,3},{3,2},{4,5},{5,4},{6,7},{7,6},{8,9},{9,8},{10,11... | collective-permute-start | bytes 196616 | tf_op jit(solution)/shard_map/ppermute | solution.py:18
  33.7 0.5 collective-permute-start.12
  34.2 0.0 collective-permute-done.9
  34.2 0.1 collective-permute-start.15
  34.3 3.3 %collective-permute-done.13 = bf16[64,512]{1,0:T(8,128)(2,1)S(1)} collective-permute-done((bf16[64,512]{1,0:T(8,128)(2,1)S(1)}, bf16[64,512]{1,0:T(8,128)(2,1)S(1)}, u32[]{:S(2)}, u32[]{:S(2)}) %collective-permute-start.13) | collective-permute-done | bytes 65568 | tf_op jit(solution)/shard_map/ppermute | solution.py:18
  37.6 1.7 %collective-permute-start.16 = (bf16[64,512]{1,0:T(8,128)(2,1)S(1)}, bf16[64,512]{1,0:T(8,128)(2,1)S(1)}, u32[]{:S(2)}, u32[]{:S(2)}) collective-permute-start(bf16[64,512]{1,0:T(8,128)(2,1)S(1)} %fusion.6), channel_id=1, source_target_pairs={{0,6},{1,7},{2,0},{3,1},{4,2},{5,3},{6,4},{7,5},{8,14},{9,15},{10,... | collective-permute-start | bytes 196616 | tf_op jit(solution)/shard_map/ppermute | solution.py:23
  39.4 0.1 collective-permute-start.17
  39.5 0.8 %collective-permute-done.15 = bf16[64,512]{1,0:T(8,128)(2,1)S(1)} collective-permute-done((bf16[64,512]{1,0:T(8,128)(2,1)S(1)}, bf16[64,512]{1,0:T(8,128)(2,1)S(1)}, u32[]{:S(2)}, u32[]{:S(2)}) %collective-permute-start.15) | collective-permute-done | bytes 65568 | tf_op jit(solution)/shard_map/ppermute | solution.py:23
  40.3 2.0 %collective-permute-done.16 = bf16[64,512]{1,0:T(8,128)(2,1)S(1)} collective-permute-done((bf16[64,512]{1,0:T(8,128)(2,1)S(1)}, bf16[64,512]{1,0:T(8,128)(2,1)S(1)}, u32[]{:S(2)}, u32[]{:S(2)}) %collective-permute-start.16) | collective-permute-done | bytes 65568 | tf_op jit(solution)/shard_map/ppermute | solution.py:23
  42.3 2.8 %collective-permute-done.17 = bf16[64,512]{1,0:T(8,128)(2,1)S(1)} collective-permute-done((bf16[64,512]{1,0:T(8,128)(2,1)S(1)}, bf16[64,512]{1,0:T(8,128)(2,1)S(1)}, u32[]{:S(2)}, u32[]{:S(2)}) %collective-permute-start.17) | collective-permute-done | bytes 65568 | tf_op jit(solution)/shard_map/ppermute | solution.py:23
  45.2 1.6 %collective-permute-start.18 = (f32[64,512]{1,0:T(8,128)S(1)}, f32[64,512]{1,0:T(8,128)S(1)}, u32[]{:S(2)}, u32[]{:S(2)}) collective-permute-start(f32[64,512]{1,0:T(8,128)S(1)} %fusion.14), channel_id=1, source_target_pairs={{0,16},{8,24},{16,0},{24,8},{1,17},{9,25},{17,1},{25,9},{2,18},{10... | collective-permute-start | bytes 393224 | tf_op jit(solution)/shard_map/ppermute | solution.py:18
  46.7 3.5 %collective-permute-done.18 = f32[64,512]{1,0:T(8,128)S(1)} collective-permute-done((f32[64,512]{1,0:T(8,128)S(1)}, f32[64,512]{1,0:T(8,128)S(1)}, u32[]{:S(2)}, u32[]{:S(2)}) %collective-permute-start.18) | collective-permute-done | bytes 131104 | tf_op jit(solution)/shard_map/ppermute | solution.py:18
  50.2 0.1 collective-permute-start.19
  50.3 1.3 %copy.9 = f32[1024,256]{1,0:T(8,128)} copy(f32[1024,256]{0,1:T(8,128)S(1)} %bitcast.11) | data formatting | bytes 2097152
  51.6 0.0 collective-permute-done.19
  51.7 0.7 %pad_maximum_fusion.1 = (f32[128,256]{1,0:T(8,128)}, f32[128,256]{1,0:T(8,128)}) fusion(f32[64,512]{1,0:T(8,128)S(1)} %get-tuple-element.68, f32[64,512]{1,0:T(8,128)S(1)} %get-tuple-element.69), kind=kLoop, calls=%fused_computation.4 | loop fusion | flops 65536 | bytes 524288 | tf_op jit(solution)/shard_map/concatenate | solution.py:319
  (20 shorter events, 0.2 us)
Async XLA Ops:
  1.4 8.6 %collective-permute-start.2 = (bf16[64,512]{1,0:T(8,128)(2,1)S(1)}, bf16[64,512]{1,0:T(8,128)(2,1)S(1)}, u32[]{:S(2)}, u32[]{:S(2)}) collective-permute-start(bf16[64,512]{1,0:T(8,128)(2,1)S(1)} %fusion.15), channel_id=1, source_target_pairs={{0,6},{1,7},{2,0},{3,1},{4,2},{5,3},{6,4},{7,5},{8,14},{9,15},{10,... | collective-permute-start | bytes 196616 | tf_op jit(solution)/shard_map/ppermute | solution.py:23
  6.5 6.2 %collective-permute-start.1 = (bf16[64,512]{1,0:T(8,128)(2,1)S(1)}, bf16[64,512]{1,0:T(8,128)(2,1)S(1)}, u32[]{:S(2)}, u32[]{:S(2)}) collective-permute-start(bf16[64,512]{1,0:T(8,128)(2,1)S(1)} %fusion.15), channel_id=1, source_target_pairs={{0,2},{1,3},{2,4},{3,5},{4,6},{5,7},{6,0},{7,1},{8,10},{9,11},{10,... | collective-permute-start | bytes 196616 | tf_op jit(solution)/shard_map/ppermute | solution.py:23
  6.5 7.5 %collective-permute-start = (bf16[64,512]{1,0:T(8,128)(2,1)S(1)}, bf16[64,512]{1,0:T(8,128)(2,1)S(1)}, u32[]{:S(2)}, u32[]{:S(2)}) collective-permute-start(bf16[64,512]{1,0:T(8,128)(2,1)S(1)} %fusion.15), channel_id=1, source_target_pairs={{0,4},{1,5},{2,6},{3,7},{4,0},{5,1},{6,2},{7,3},{8,12},{9,13},{10,... | collective-permute-start | bytes 196616 | tf_op jit(solution)/shard_map/ppermute | solution.py:23
  14.0 10.5 %copy-start = (bf16[1024,256]{1,0:T(8,128)(2,1)S(1)}, bf16[1024,256]{1,0:T(8,128)(2,1)}, u32[]{:S(2)}) copy-start(bf16[1024,256]{1,0:T(8,128)(2,1)} %refs_0_.7) | copy-start | bytes 1572868
  14.0 10.4 %copy-start.1 = (bf16[1024,256]{1,0:T(8,128)(2,1)S(1)}, bf16[1024,256]{1,0:T(8,128)(2,1)}, u32[]{:S(2)}) copy-start(bf16[1024,256]{1,0:T(8,128)(2,1)} %refs_1_.7) | copy-start | bytes 1572868
  14.0 5.1 %collective-permute-start.7 = (bf16[256,512]{1,0:T(8,128)(2,1)S(1)}, bf16[256,512]{1,0:T(8,128)(2,1)S(1)}, u32[]{:S(2)}, u32[]{:S(2)}) collective-permute-start(bf16[256,512]{1,0:T(8,128)(2,1)S(1)} %pad_maximum_fusion.refs_2_), channel_id=1, source_target_pairs={{0,8},{8,0},{16,24},{24,16},{1,9},{9,1},{17,25},{25,17},{2,10},{10... | collective-permute-start | bytes 786440 | tf_op jit(solution)/shard_map/ppermute | solution.py:18
  14.1 5.8 %collective-permute-start.3 = (bf16[64,512]{1,0:T(8,128)(2,1)S(1)}, bf16[64,512]{1,0:T(8,128)(2,1)S(1)}, u32[]{:S(2)}, u32[]{:S(2)}) collective-permute-start(bf16[64,512]{1,0:T(8,128)(2,1)S(1)} %fusion.15), channel_id=1, source_target_pairs={{0,1},{1,0},{2,3},{3,2},{4,5},{5,4},{6,7},{7,6},{8,9},{9,8},{10,11... | collective-permute-start | bytes 196616 | tf_op jit(solution)/shard_map/ppermute | solution.py:18
  15.7 5.0 %collective-permute-start.5 = (bf16[64,512]{1,0:T(8,128)(2,1)S(1)}, bf16[64,512]{1,0:T(8,128)(2,1)S(1)}, u32[]{:S(2)}, u32[]{:S(2)}) collective-permute-start(bf16[64,512]{1,0:T(8,128)(2,1)S(1)} %collective-permute-done.1), channel_id=1, source_target_pairs={{0,1},{1,0},{2,3},{3,2},{4,5},{5,4},{6,7},{7,6},{8,9},{9,8},{10,11... | collective-permute-start | bytes 196616 | tf_op jit(solution)/shard_map/ppermute | solution.py:18
  16.2 5.9 %collective-permute-start.4 = (bf16[64,512]{1,0:T(8,128)(2,1)S(1)}, bf16[64,512]{1,0:T(8,128)(2,1)S(1)}, u32[]{:S(2)}, u32[]{:S(2)}) collective-permute-start(bf16[64,512]{1,0:T(8,128)(2,1)S(1)} %collective-permute-done), channel_id=1, source_target_pairs={{0,1},{1,0},{2,3},{3,2},{4,5},{5,4},{6,7},{7,6},{8,9},{9,8},{10,11... | collective-permute-start | bytes 196616 | tf_op jit(solution)/shard_map/ppermute | solution.py:18
  17.7 5.1 %collective-permute-start.6 = (bf16[64,512]{1,0:T(8,128)(2,1)S(1)}, bf16[64,512]{1,0:T(8,128)(2,1)S(1)}, u32[]{:S(2)}, u32[]{:S(2)}) collective-permute-start(bf16[64,512]{1,0:T(8,128)(2,1)S(1)} %collective-permute-done.2), channel_id=1, source_target_pairs={{0,1},{1,0},{2,3},{3,2},{4,5},{5,4},{6,7},{7,6},{8,9},{9,8},{10,11... | collective-permute-start | bytes 196616 | tf_op jit(solution)/shard_map/ppermute | solution.py:18
  22.8 1.6 %collective-permute-start.8 = (bf16[256,512]{1,0:T(8,128)(2,1)S(1)}, bf16[256,512]{1,0:T(8,128)(2,1)S(1)}, u32[]{:S(2)}, u32[]{:S(2)}) collective-permute-start(bf16[256,512]{1,0:T(8,128)(2,1)S(1)} %constant_dynamic-update-slice_fusion.refs_2_), channel_id=1, source_target_pairs={{0,8},{8,0},{16,24},{24,16},{1,9},{9,1},{17,25},{25,17},{2,10},{10... | collective-permute-start | bytes 786440 | tf_op jit(solution)/shard_map/ppermute | solution.py:18
  26.7 2.4 %collective-permute-start.10 = (f32[256,512]{1,0:T(8,128)S(1)}, f32[256,512]{1,0:T(8,128)S(1)}, u32[]{:S(2)}, u32[]{:S(2)}) collective-permute-start(f32[256,512]{1,0:T(8,128)S(1)} %get-tuple-element.55), channel_id=1, source_target_pairs={{0,8},{8,0},{16,24},{24,16},{1,9},{9,1},{17,25},{25,17},{2,10},{10... | collective-permute-start | bytes 1572872 | tf_op jit(solution)/shard_map/ppermute | solution.py:18
  27.7 6.5 %collective-permute-start.9 = (f32[256,512]{1,0:T(8,128)S(1)}, f32[256,512]{1,0:T(8,128)S(1)}, u32[]{:S(2)}, u32[]{:S(2)}) collective-permute-start(f32[256,512]{1,0:T(8,128)S(1)} %get-tuple-element.53), channel_id=1, source_target_pairs={{0,8},{8,0},{16,24},{24,16},{1,9},{9,1},{17,25},{25,17},{2,10},{10... | collective-permute-start | bytes 1572872 | tf_op jit(solution)/shard_map/ppermute | solution.py:18
  29.1 5.1 %collective-permute-start.14 = (bf16[64,512]{1,0:T(8,128)(2,1)S(1)}, bf16[64,512]{1,0:T(8,128)(2,1)S(1)}, u32[]{:S(2)}, u32[]{:S(2)}) collective-permute-start(bf16[64,512]{1,0:T(8,128)(2,1)S(1)} %get-tuple-element.63), channel_id=1, source_target_pairs={{0,1},{1,0},{2,3},{3,2},{4,5},{5,4},{6,7},{7,6},{8,9},{9,8},{10,11... | collective-permute-start | bytes 196616 | tf_op jit(solution)/shard_map/ppermute | solution.py:18
  31.6 7.9 %collective-permute-start.11 = (bf16[64,512]{1,0:T(8,128)(2,1)S(1)}, bf16[64,512]{1,0:T(8,128)(2,1)S(1)}, u32[]{:S(2)}, u32[]{:S(2)}) collective-permute-start(bf16[64,512]{1,0:T(8,128)(2,1)S(1)} %get-tuple-element.62), channel_id=1, source_target_pairs={{0,1},{1,0},{2,3},{3,2},{4,5},{5,4},{6,7},{7,6},{8,9},{9,8},{10,11... | collective-permute-start | bytes 196616 | tf_op jit(solution)/shard_map/ppermute | solution.py:18
  32.2 5.4 %collective-permute-start.13 = (bf16[64,512]{1,0:T(8,128)(2,1)S(1)}, bf16[64,512]{1,0:T(8,128)(2,1)S(1)}, u32[]{:S(2)}, u32[]{:S(2)}) collective-permute-start(bf16[64,512]{1,0:T(8,128)(2,1)S(1)} %get-tuple-element.64), channel_id=1, source_target_pairs={{0,1},{1,0},{2,3},{3,2},{4,5},{5,4},{6,7},{7,6},{8,9},{9,8},{10,11... | collective-permute-start | bytes 196616 | tf_op jit(solution)/shard_map/ppermute | solution.py:18
  33.7 5.7 %collective-permute-start.12 = (bf16[64,512]{1,0:T(8,128)(2,1)S(1)}, bf16[64,512]{1,0:T(8,128)(2,1)S(1)}, u32[]{:S(2)}, u32[]{:S(2)}) collective-permute-start(bf16[64,512]{1,0:T(8,128)(2,1)S(1)} %get-tuple-element.65), channel_id=1, source_target_pairs={{0,1},{1,0},{2,3},{3,2},{4,5},{5,4},{6,7},{7,6},{8,9},{9,8},{10,11... | collective-permute-start | bytes 196616 | tf_op jit(solution)/shard_map/ppermute | solution.py:18
  34.2 6.1 %collective-permute-start.15 = (bf16[64,512]{1,0:T(8,128)(2,1)S(1)}, bf16[64,512]{1,0:T(8,128)(2,1)S(1)}, u32[]{:S(2)}, u32[]{:S(2)}) collective-permute-start(bf16[64,512]{1,0:T(8,128)(2,1)S(1)} %fusion.3), channel_id=1, source_target_pairs={{0,2},{1,3},{2,4},{3,5},{4,6},{5,7},{6,0},{7,1},{8,10},{9,11},{10,... | collective-permute-start | bytes 196616 | tf_op jit(solution)/shard_map/ppermute | solution.py:23
  37.6 4.7 %collective-permute-start.16 = (bf16[64,512]{1,0:T(8,128)(2,1)S(1)}, bf16[64,512]{1,0:T(8,128)(2,1)S(1)}, u32[]{:S(2)}, u32[]{:S(2)}) collective-permute-start(bf16[64,512]{1,0:T(8,128)(2,1)S(1)} %fusion.6), channel_id=1, source_target_pairs={{0,6},{1,7},{2,0},{3,1},{4,2},{5,3},{6,4},{7,5},{8,14},{9,15},{10,... | collective-permute-start | bytes 196616 | tf_op jit(solution)/shard_map/ppermute | solution.py:23
  39.4 5.7 %collective-permute-start.17 = (bf16[64,512]{1,0:T(8,128)(2,1)S(1)}, bf16[64,512]{1,0:T(8,128)(2,1)S(1)}, u32[]{:S(2)}, u32[]{:S(2)}) collective-permute-start(bf16[64,512]{1,0:T(8,128)(2,1)S(1)} %fusion.9), channel_id=1, source_target_pairs={{0,4},{1,5},{2,6},{3,7},{4,0},{5,1},{6,2},{7,3},{8,12},{9,13},{10,... | collective-permute-start | bytes 196616 | tf_op jit(solution)/shard_map/ppermute | solution.py:23
  45.2 5.0 %collective-permute-start.18 = (f32[64,512]{1,0:T(8,128)S(1)}, f32[64,512]{1,0:T(8,128)S(1)}, u32[]{:S(2)}, u32[]{:S(2)}) collective-permute-start(f32[64,512]{1,0:T(8,128)S(1)} %fusion.14), channel_id=1, source_target_pairs={{0,16},{8,24},{16,0},{24,8},{1,17},{9,25},{17,1},{25,9},{2,18},{10... | collective-permute-start | bytes 393224 | tf_op jit(solution)/shard_map/ppermute | solution.py:18
  50.2 1.4 %collective-permute-start.19 = (f32[64,512]{1,0:T(8,128)S(1)}, f32[64,512]{1,0:T(8,128)S(1)}, u32[]{:S(2)}, u32[]{:S(2)}) collective-permute-start(f32[64,512]{1,0:T(8,128)S(1)} %add.72), channel_id=1, source_target_pairs={{0,8},{8,0},{16,24},{24,16},{1,9},{9,1},{17,25},{25,17},{2,10},{10... | collective-permute-start | bytes 393224 | tf_op jit(solution)/shard_map/ppermute | solution.py:18
